TPU v7x, 512 devices: a whole 4x8x8 slice. The times are simulated.
512 devices in a mesh: mem: 32 (over y, x), space: 16 (over z, core).
Axes of the slice: x: 4, y: 8, z: 8, core: 2. Of those that a mesh axis runs over, the one named last changes fastest.
Arguments:
- ensemble: float32 [384, 3, 64, 1024], P('mem', None, 'space'), may hold values from -1.8 to 1.8
- sea_depth: float32 [64, 1024], P('space'), may hold values from 0.5 to 2
- ocean_mask: int32 [64, 1024], P('space'), may hold values 0 or 1
- observed_cells: int32 [16, 128], P('space'), may hold values from 0 to 4095
- observed_values: float32 [16, 128], P('space'), may hold values from -6 to 6
- observed_error: float32 [16, 128], P('space'), may hold values from 0.5 to 2
Outputs:
- analysis: float32 [384, 3, 64, 1024], P('mem', None, 'space')
Inputs may be any that keep to these rules, and one draw needn't show every extreme that they name: `observed_cells`: indices are local to the slab; an observation may repeat a cell.
All inputs are finite; a program needn't handle non-finite values. No bound on the sum of `ocean_mask` on one device may be relied on, other than what follows from the above.
Results may differ from a plain program's by a relative error of at most 0.00021.
Values sent between devices are 32-bit elements; how exact they have to be, the bound alone decides.
No kernel may reach another device: no remote copies, remote signals or barrier semaphores. Data moves between devices by JAX's collectives and lax.ppermute only.
A program may use at most 64 MiB of HBM per device.

v0:
```python
import functools

import jax
import jax.numpy as jnp
from jax import lax
from jax.experimental import pallas as pl
from jax.experimental.pallas import tpu as pltpu
from jax.sharding import Mesh
from jax.sharding import PartitionSpec as P

STEPS = 3
NS_ITERS = 6
MEM = ("mem_0", "mem_1")

GRAV = 1.0
DT = 0.3
VISC = 0.1

LANES = 128
GROUP = 16
HALO = 2 * STEPS


def ring(axis, turn):
    count = lax.axis_size(axis)
    return [(i, (i + turn) % count) for i in range(count)]


def halves(x):
    top = x.astype(jnp.bfloat16)
    return top, (x - top.astype(jnp.float32)).astype(jnp.bfloat16)


def product(a, b, contract=((1,), (0,))):
    left = jnp.concatenate([a[0], a[0], a[1]], axis=contract[0][0])
    right = jnp.concatenate([b[0], b[1], b[0]], axis=contract[1][0])
    return lax.dot_general(left, right, (contract, ((), ())), preferred_element_type=jnp.float32)


def room(mebibytes):
    return pltpu.CompilerParams(vmem_limit_bytes=mebibytes << 20)


def forecast_kernel(cells, wide_ref, coriolis_ref, out_ref, a_ref, b_ref, fresh_ref):
    rows, _, columns = wide_ref.shape
    members = a_ref.shape[2]
    rows_here = rows - 2 * HALO
    coriolis = coriolis_ref[...] * DT
    parts = [slice(at, min(at + 8, members)) for at in range(0, members, 8)]
    depth_at = slice(3 * members, 3 * members + 1)
    ocean_at = slice(3 * members + 1, 3 * members + 2)

    def north(x):
        return pltpu.roll(x, columns - 1, 1)

    def south(x):
        return pltpu.roll(x, 1, 1)

    def unpack(r, carry):
        for f in range(3):
            b_ref[f, r] = wide_ref[r, f * members : (f + 1) * members, :]
        return carry

    lax.fori_loop(0, rows, unpack, 0)

    for step in range(STEPS):
        source, target = (b_ref, a_ref) if step % 2 == 0 else (a_ref, b_ref)
        low = 2 * step

        def height_row(r, carry, source=source):
            depth_above = wide_ref[r + 1, depth_at]
            depth_below = wide_ref[r - 1, depth_at]
            depth = wide_ref[r, depth_at]
            for m in parts:
                above = (depth_above + source[0, r + 1, m]) * source[1, r + 1, m]
                below = (depth_below + source[0, r - 1, m]) * source[1, r - 1, m]
                height = source[0, r, m]
                across = (depth + height) * source[2, r, m]
                fresh_ref[r, m] = height - (0.5 * DT) * (
                    (above - below) + (north(across) - south(across))
                )
            return carry

        lax.fori_loop(low + 1, rows - low - 1, height_row, 0)

        def flow_row(r, carry, source=source, target=target):
            ocean = wide_ref[r, ocean_at]
            for m in parts:
                u, v = source[1, r, m], source[2, r, m]
                ue, uw = source[1, r + 1, m], source[1, r - 1, m]
                un, us = north(u), south(u)
                tend = GRAV * (fresh_ref[r + 1, m] - fresh_ref[r - 1, m])
                tend = tend + u * (ue - uw) + v * (un - us)
                new = (1.0 - 4.0 * DT * VISC) * u - (0.5 * DT) * tend + coriolis * v
                target[1, r, m] = (new + (DT * VISC) * ((ue + uw) + (un + us))) * ocean
                fresh = fresh_ref[r, m]
                target[0, r, m] = fresh
                ve, vw = source[2, r + 1, m], source[2, r - 1, m]
                vn, vs = north(v), south(v)
                tend = GRAV * (north(fresh) - south(fresh)) + u * (ve - vw) + v * (vn - vs)
                new = (1.0 - 4.0 * DT * VISC) * v - (0.5 * DT) * tend - coriolis * u
                target[2, r, m] = (new + (DT * VISC) * ((ve + vw) + (vn + vs))) * ocean
            return carry

        lax.fori_loop(low + 2, rows - low - 2, flow_row, 0)
    source = target

    lane = lax.broadcasted_iota(jnp.int32, (members, LANES), 1)

    def pick(o, found):
        cell = cells[0, o]
        row = cell // columns
        column = cell % columns
        start = pl.multiple_of((column // LANES) * LANES, LANES)
        block = source[0, HALO + row, :, pl.ds(start, LANES)]
        turned = pltpu.roll(block, (o - column % LANES + LANES) % LANES, 1)
        return jnp.where(lane == o, turned, found)

    picks = lax.fori_loop(0, LANES, pick, jnp.zeros((members, LANES), jnp.float32), unroll=8)
    per_row = columns // LANES
    spare = members // 3
    for f in range(3):
        part = picks[f * spare : (f + 1) * spare]
        for r in range(rows_here):
            for c in range(per_row):
                d = r * per_row + c
                out_ref[d, f * GROUP : f * GROUP + members, :] = source[
                    f, HALO + r, :, c * LANES : (c + 1) * LANES
                ]
                out_ref[d, f * GROUP + members : (f + 1) * GROUP, :] = part


def forecast(cells, wide, coriolis, members, blocks):
    rows, _, columns = wide.shape
    vmem = pl.BlockSpec(memory_space=pltpu.VMEM)
    return pl.pallas_call(
        forecast_kernel,
        out_shape=jax.ShapeDtypeStruct((blocks, 3 * GROUP, LANES), jnp.float32),
        in_specs=[pl.BlockSpec(memory_space=pltpu.SMEM), vmem, vmem],
        out_specs=vmem,
        scratch_shapes=[
            pltpu.VMEM((3, rows, members, columns), jnp.float32),
            pltpu.VMEM((3, rows, members, columns), jnp.float32),
            pltpu.VMEM((rows, members, columns), jnp.float32),
        ],
        compiler_params=room(16),
        name="forecast",
    )(cells, wide, coriolis)


def gram_kernel(own, gathered_ref, value_ref, error_ref, out_ref, picks_ref, stack_ref):
    devices = gathered_ref.shape[0]
    members = 12
    spare = members // 3
    for d in range(devices):
        for f in range(3):
            at = d * members + f * spare
            picks_ref[at : at + spare, :] = gathered_ref[
                d, f * GROUP + members : (f + 1) * GROUP, :
            ]
    picks = picks_ref[...]
    hmean = jnp.mean(picks, axis=0, keepdims=True)
    scaled = (picks - hmean) / error_ref[...]
    misfit = (value_ref[...] - hmean) / error_ref[...]
    scaled_halves = halves(scaled)
    gram = product(scaled_halves, scaled_halves, ((1,), (1,)))
    drive = product(
        halves(jnp.broadcast_to(misfit, (8, LANES))), scaled_halves, ((1,), (1,))
    )
    n = LANES
    row = lax.broadcasted_iota(jnp.int32, (n, n), 0)
    column = lax.broadcasted_iota(jnp.int32, (n, n), 1)
    middle = gram[n : 2 * n, n : 2 * n]
    stack_ref[0:n] = gram[0:n, n : 2 * n]
    stack_ref[n : 2 * n] = gram[0:n, 2 * n :]
    stack_ref[2 * n : 3 * n] = gram[n : 2 * n, 2 * n :]
    stack_ref[3 * n : 4 * n] = jnp.where(row <= column, gram[0:n, 0:n], middle)
    stack_ref[4 * n : 5 * n] = gram[2 * n :, 2 * n :]
    stack_ref[5 * n :] = jnp.zeros((n, n), jnp.float32)
    diagonal = jnp.sum(jnp.where(row == column, middle, 0.0), axis=0, keepdims=True)
    stack_ref[5 * n : 5 * n + 1] = diagonal
    for k in range(3):
        stack_ref[5 * n + 8 * (k + 1) : 5 * n + 8 * (k + 2)] = drive[:, k * n : (k + 1) * n]
    size = out_ref.shape[1]
    piece = stack_ref[pl.ds(pl.multiple_of(own[0] * size, 8), size), :]
    out_ref[...] = jnp.broadcast_to(piece[None], out_ref.shape)


def gram_piece(own, gathered, value, error, slabs):
    devices = gathered.shape[0]
    ens = 3 * LANES
    size = 6 * LANES // devices
    vmem = pl.BlockSpec(memory_space=pltpu.VMEM)
    return pl.pallas_call(
        gram_kernel,
        out_shape=jax.ShapeDtypeStruct((slabs, size, LANES), jnp.float32),
        in_specs=[pl.BlockSpec(memory_space=pltpu.SMEM), vmem, vmem, vmem],
        out_specs=vmem,
        scratch_shapes=[
            pltpu.VMEM((ens, LANES), jnp.float32),
            pltpu.VMEM((6 * LANES, LANES), jnp.float32),
        ],
        compiler_params=room(8),
        name="gram",
    )(own, gathered, value, error)


def total_kernel(parts_ref, out_ref):
    total = jnp.sum(parts_ref[...], axis=0, keepdims=True)
    out_ref[...] = jnp.broadcast_to(total, out_ref.shape)


def total_piece(parts, devices):
    vmem = pl.BlockSpec(memory_space=pltpu.VMEM)
    return pl.pallas_call(
        total_kernel,
        out_shape=jax.ShapeDtypeStruct((devices, *parts.shape[1:]), jnp.float32),
        in_specs=[vmem],
        out_specs=vmem,
        compiler_params=room(8),
        name="total",
    )(parts)


def analysis_kernel(stack_ref, gathered_ref, out_ref, gram_ref, field_ref):
    n = LANES
    ens = 3 * n
    devices = gathered_ref.shape[0]
    members = ens // devices
    row = lax.broadcasted_iota(jnp.int32, (n, n), 0)
    column = lax.broadcasted_iota(jnp.int32, (n, n), 1)

    def block(k):
        return stack_ref[k * n : (k + 1) * n]

    for k, (i, j) in enumerate(((0, 1), (0, 2), (1, 2))):
        gram_ref[i * n : (i + 1) * n, j * n : (j + 1) * n] = block(k)
        gram_ref[j * n : (j + 1) * n, i * n : (i + 1) * n] = block(k).T
    both = block(3)
    upper = jnp.where(row < column, both, 0.0)
    gram_ref[0:n, 0:n] = upper + upper.T + jnp.where(row == column, both, 0.0)
    lower = jnp.where(row > column, both, 0.0)
    middle = jnp.where(row == column, stack_ref[5 * n : 5 * n + 1], 0.0)
    gram_ref[n : 2 * n, n : 2 * n] = lower + lower.T + middle
    gram_ref[2 * n :, 2 * n :] = block(4)
    drive = jnp.concatenate(
        [stack_ref[5 * n + 8 * (k + 1) : 5 * n + 8 * (k + 1) + 1] for k in range(3)], axis=1
    )

    same = lax.broadcasted_iota(jnp.int32, (ens, ens), 0) == lax.broadcasted_iota(
        jnp.int32, (ens, ens), 1
    )
    identity = jnp.where(same, 1.0, 0.0)
    system = identity + gram_ref[...] * (1.0 / (ens - 1))
    norm_scale = jnp.sqrt(jnp.sum(system * system, keepdims=True))
    iterate = system / norm_scale
    inverse = 1.5 * identity - 0.5 * iterate
    iterate = product(halves(iterate), halves(inverse))
    for sweep in range(1, NS_ITERS):
        iterate_halves = halves(iterate)
        inverse_halves = halves(inverse)
        factor_halves = halves(1.5 * identity - 0.5 * product(inverse_halves, iterate_halves))
        inverse = product(inverse_halves, factor_halves)
        if sweep + 1 < NS_ITERS:
            iterate = product(iterate_halves, factor_halves)
    weights = inverse / jnp.sqrt(norm_scale)
    pulled = jnp.sum(weights * drive, axis=1, keepdims=True)
    mean_weight = jnp.sum(weights * pulled, axis=0, keepdims=True) * (1.0 / (ens - 1))
    combined = halves(weights + mean_weight)

    for f in range(3):
        for d in range(devices):
            field_ref[f, d * members : (d + 1) * members, :] = gathered_ref[
                d, f * GROUP : f * GROUP + members, :
            ]
    for f in range(3):
        field = field_ref[f]
        center = jnp.mean(field, axis=0, keepdims=True)
        field_ref[f] = center + product(combined, halves(field - center))
    for f in range(3):
        for d in range(devices):
            out_ref[d, f * members : (f + 1) * members, :] = field_ref[
                f, d * members : (d + 1) * members, :
            ]


def analysis(stack, gathered):
    devices = gathered.shape[0]
    ens = 3 * LANES
    vmem = pl.BlockSpec(memory_space=pltpu.VMEM)
    return pl.pallas_call(
        analysis_kernel,
        out_shape=jax.ShapeDtypeStruct((devices, 3 * ens // devices, LANES), jnp.float32),
        in_specs=[vmem, vmem],
        out_specs=vmem,
        scratch_shapes=[
            pltpu.VMEM((ens, ens), jnp.float32),
            pltpu.VMEM((3, ens, LANES), jnp.float32),
        ],
        compiler_params=room(16),
        name="analysis",
    )(stack, gathered)


def local(ensemble, sea_depth, ocean_mask, observed_cells, observed_values, observed_error):
    local_members, fields, rows_here, columns = ensemble.shape
    devices = lax.axis_size(MEM)
    slabs = lax.axis_size("space")
    coriolis = 0.05 + 0.1 * jnp.arange(columns, dtype=jnp.float32)[None] / columns
    still = jnp.stack([sea_depth, ocean_mask.astype(jnp.float32)], axis=1)
    moving = ensemble.transpose(2, 1, 0, 3).reshape(rows_here, fields * local_members, columns)
    planes = jnp.concatenate([moving, still], axis=1)
    edge = HALO - rows_here
    before = lax.ppermute(planes, "space", ring("space", 1))
    after = lax.ppermute(planes, "space", ring("space", -1))
    far_before = lax.ppermute(planes[rows_here - edge :], "space", ring("space", 2))
    far_after = lax.ppermute(planes[:edge], "space", ring("space", -2))
    wide = jnp.concatenate([far_before, before, planes, after, far_after], axis=0)
    sent = forecast(observed_cells, wide, coriolis, local_members, devices)
    gathered = lax.all_to_all(sent, MEM, 0, 0, tiled=True)
    own = lax.axis_index(MEM).astype(jnp.int32).reshape(1)
    parts = gram_piece(own, gathered, observed_values, observed_error, slabs)
    parts = lax.all_to_all(parts, "space", 0, 0, tiled=True)
    pieces = lax.all_to_all(total_piece(parts, devices), MEM, 0, 0, tiled=True)
    result = analysis(pieces.reshape(-1, LANES), gathered)
    returned = lax.all_to_all(result, MEM, 0, 0, tiled=True)
    returned = returned.reshape(rows_here, columns // LANES, fields, local_members, LANES)
    return returned.transpose(3, 2, 0, 1, 4).reshape(ensemble.shape)


def solution(mesh):
    finer = Mesh(mesh.devices.reshape(8, 4, mesh.shape["space"]), ("mem_0", "mem_1", "space"))
    return jax.shard_map(
        local,
        mesh=finer,
        in_specs=(
            P(MEM, None, "space", None),
            P("space", None),
            P("space", None),
            P("space", None),
            P("space", None),
            P("space", None),
        ),
        out_specs=P(MEM, None, "space", None),
        check_vma=False,
    )
```

profile of v0, /device:TPU:8, one launch (start us, length us, event | category | flops | bytes accessed | tf_op | source)
XLA Modules:
  0.0 144.2 jit_solution(5532665072570216598)
XLA Ops:
  0.0 1.1 copy.13
  1.1 0.3 copy.14
  1.5 0.7 convert_element_type.3
  2.2 0.7 stack.6
  3.0 0.4 copy.15
  3.5 4.3 %collective-permute-start = (f32[2,38,1024]{2,1,0:T(8,128)S(1)}, f32[2,38,1024]{2,1,0:T(8,128)S(1)}, u32[]{:S(2)}, u32[]{:S(2)}) collective-permute-start(f32[2,38,1024]{2,1,0:T(8,128)S(1)} %get-tuple-element.6), channel_id=1, source_target_pairs={{0,2},{1,3},{2,4},{3,5},{4,6},{5,7},{6,8},{7,9},{8,10},{9,11},{10,... | collective-permute-start | bytes 933896 | tf_op jit(solution)/shard_map/ppermute | solution.py:316
  7.8 6.1 %collective-permute-start.2 = (f32[4,38,1024]{2,0,1:T(4,128)S(1)}, f32[4,38,1024]{2,0,1:T(4,128)S(1)}, u32[]{:S(2)}, u32[]{:S(2)}) collective-permute-start(f32[4,38,1024]{2,0,1:T(4,128)S(1)} %copy.15), channel_id=1, source_target_pairs={{0,15},{1,0},{2,1},{3,2},{4,3},{5,4},{6,5},{7,6},{8,7},{9,8},{10,9... | collective-permute-start | bytes 1867784 | tf_op jit(solution)/shard_map/ppermute | solution.py:315
  14.0 4.2 %collective-permute-start.3 = (f32[2,38,1024]{2,1,0:T(8,128)S(1)}, f32[2,38,1024]{2,1,0:T(8,128)S(1)}, u32[]{:S(2)}, u32[]{:S(2)}) collective-permute-start(f32[2,38,1024]{2,1,0:T(8,128)S(1)} %get-tuple-element.5), channel_id=1, source_target_pairs={{0,14},{1,15},{2,0},{3,1},{4,2},{5,3},{6,4},{7,5},{8,6},{9,7},{10,... | collective-permute-start | bytes 933896 | tf_op jit(solution)/shard_map/ppermute | solution.py:317
  18.2 4.9 %collective-permute-done = f32[2,38,1024]{2,1,0:T(8,128)S(1)} collective-permute-done((f32[2,38,1024]{2,1,0:T(8,128)S(1)}, f32[2,38,1024]{2,1,0:T(8,128)S(1)}, u32[]{:S(2)}, u32[]{:S(2)}) %collective-permute-start) | collective-permute-done | bytes 311328 | tf_op jit(solution)/shard_map/ppermute | solution.py:316
  23.1 0.3 collective-permute-done.1
  23.4 0.4 copy_dynamic-update-slice_fusion.1
  23.8 1.4 collective-permute-done.2
  25.2 0.4 copy_dynamic-update-slice_fusion
  25.6 3.1 %collective-permute-done.3 = f32[2,38,1024]{2,1,0:T(8,128)S(1)} collective-permute-done((f32[2,38,1024]{2,1,0:T(8,128)S(1)}, f32[2,38,1024]{2,1,0:T(8,128)S(1)}, u32[]{:S(2)}, u32[]{:S(2)}) %collective-permute-start.3) | collective-permute-done | bytes 311328 | tf_op jit(solution)/shard_map/ppermute | solution.py:317
  28.8 12.2 %forecast.1 = f32[32,48,128]{2,1,0:T(8,128)} custom-call(s32[1,128]{1,0:T(1,128)S(1)} %copy-done, f32[16,38,1024]{2,1,0:T(8,128)S(1)} %constant_dynamic-update-slice_fusion.wide_ref, f32[1,1024]{1,0:T(1,128)S(1)} %multiply_add_fusion.coriolis_ref), custom_call_target="tpu_custom_call" | custom-call | tf_op jit(solution)/shard_map/forecast/pallas_call | solution.py:136
  41.0 10.2 %all-to-all-start = ((f32[32,48,128]{2,1,0:T(8,128)}), f32[32,48,128]{2,1,0:T(8,128)S(1)}, u32[]{:S(2)}, u32[]{:S(2)}) async-start(f32[32,48,128]{2,1,0:T(8,128)} %forecast.1), calls=%async_computation | async-start | bytes 1572864 | tf_op jit(solution)/shard_map/all_to_all | solution.py:320
  51.2 21.4 %all-to-all-done.gathered_ref = f32[32,48,128]{2,1,0:T(8,128)S(1)} async-done(((f32[32,48,128]{2,1,0:T(8,128)}), f32[32,48,128]{2,1,0:T(8,128)S(1)}, u32[]{:S(2)}, u32[]{:S(2)}) %all-to-all-start) | async-done | bytes 786464 | tf_op jit(solution)/shard_map/all_to_all | solution.py:320
  72.5 0.5 gram.1
  73.1 14.6 %all_to_all.20.parts_ref = f32[16,24,128]{2,1,0:T(8,128)S(1)} all-to-all(f32[16,24,128]{2,1,0:T(8,128)S(1)} %gram.1), channel_id=1, replica_groups=mesh['mem_0'=8,'mem_1'=4,'space'=16] {'space'}, dimensions={0} | all-to-all | bytes 393216 | tf_op jit(solution)/shard_map/all_to_all | solution.py:323
  87.7 20.8 %all_to_all.21 = f32[32,24,128]{2,1,0:T(8,128)S(1)} all-to-all(f32[32,24,128]{2,1,0:T(8,128)S(1)} %total.1), channel_id=1, replica_groups=mesh['mem_0'=8,'mem_1'=4,'space'=16] {'mem_0','mem_1'}, dimensions={0} | all-to-all | bytes 786432 | tf_op jit(solution)/shard_map/all_to_all | solution.py:324
  108.5 10.2 %analysis.1 = f32[32,36,128]{2,1,0:T(8,128)S(1)} custom-call(f32[768,128]{1,0:T(8,128)S(1)} %bitcast.11, f32[32,48,128]{2,1,0:T(8,128)S(1)} %all-to-all-done.gathered_ref), custom_call_target="tpu_custom_call" | custom-call | tf_op jit(solution)/shard_map/analysis/pallas_call | solution.py:291
  118.7 24.3 %all_to_all.22 = f32[32,36,128]{2,1,0:T(8,128)S(1)} all-to-all(f32[32,36,128]{2,1,0:T(8,128)S(1)} %analysis.1), channel_id=1, replica_groups=mesh['mem_0'=8,'mem_1'=4,'space'=16] {'mem_0','mem_1'}, dimensions={0} | all-to-all | bytes 1179648 | tf_op jit(solution)/shard_map/all_to_all | solution.py:326
  143.1 0.2 reshape.32
  143.3 0.9 copy.20
  (16 shorter events, 0.5 us)
Async XLA Ops:
  3.4 19.9 %collective-permute-start.1 = (f32[4,38,1024]{2,0,1:T(4,128)S(1)}, f32[4,38,1024]{2,0,1:T(4,128)S(1)}, u32[]{:S(2)}, u32[]{:S(2)}) collective-permute-start(f32[4,38,1024]{2,0,1:T(4,128)S(1)} %copy.15), channel_id=1, source_target_pairs={{0,1},{1,2},{2,3},{3,4},{4,5},{5,6},{6,7},{7,8},{8,9},{9,10},{10,1... | collective-permute-start | bytes 1867784 | tf_op jit(solution)/shard_map/ppermute | solution.py:314
  3.5 25.2 %copy-start = (s32[1,128]{1,0:T(1,128)S(1)}, s32[1,128]{1,0:T(1,128)}, u32[]{:S(2)}) copy-start(s32[1,128]{1,0:T(1,128)} %cells.1) | copy-start | bytes 1540
  3.5 19.5 %collective-permute-start = (f32[2,38,1024]{2,1,0:T(8,128)S(1)}, f32[2,38,1024]{2,1,0:T(8,128)S(1)}, u32[]{:S(2)}, u32[]{:S(2)}) collective-permute-start(f32[2,38,1024]{2,1,0:T(8,128)S(1)} %get-tuple-element.6), channel_id=1, source_target_pairs={{0,2},{1,3},{2,4},{3,5},{4,6},{5,7},{6,8},{7,9},{8,10},{9,11},{10,... | collective-permute-start | bytes 933896 | tf_op jit(solution)/shard_map/ppermute | solution.py:316
  7.8 17.4 %collective-permute-start.2 = (f32[4,38,1024]{2,0,1:T(4,128)S(1)}, f32[4,38,1024]{2,0,1:T(4,128)S(1)}, u32[]{:S(2)}, u32[]{:S(2)}) collective-permute-start(f32[4,38,1024]{2,0,1:T(4,128)S(1)} %copy.15), channel_id=1, source_target_pairs={{0,15},{1,0},{2,1},{3,2},{4,3},{5,4},{6,5},{7,6},{8,7},{9,8},{10,9... | collective-permute-start | bytes 1867784 | tf_op jit(solution)/shard_map/ppermute | solution.py:315
  14.0 14.8 %collective-permute-start.3 = (f32[2,38,1024]{2,1,0:T(8,128)S(1)}, f32[2,38,1024]{2,1,0:T(8,128)S(1)}, u32[]{:S(2)}, u32[]{:S(2)}) collective-permute-start(f32[2,38,1024]{2,1,0:T(8,128)S(1)} %get-tuple-element.5), channel_id=1, source_target_pairs={{0,14},{1,15},{2,0},{3,1},{4,2},{5,3},{6,4},{7,5},{8,6},{9,7},{10,... | collective-permute-start | bytes 933896 | tf_op jit(solution)/shard_map/ppermute | solution.py:317
  28.8 43.8 %copy-start.1 = (f32[1,128]{1,0:T(1,128)S(1)}, f32[1,128]{1,0:T(1,128)}, u32[]{:S(2)}) copy-start(f32[1,128]{1,0:T(1,128)} %value_ref.1) | copy-start | bytes 1540
  28.8 43.8 %copy-start.2 = (f32[1,128]{1,0:T(1,128)S(1)}, f32[1,128]{1,0:T(1,128)}, u32[]{:S(2)}) copy-start(f32[1,128]{1,0:T(1,128)} %error_ref.1) | copy-start | bytes 1540
  41.0 31.6 %all-to-all-start = ((f32[32,48,128]{2,1,0:T(8,128)}), f32[32,48,128]{2,1,0:T(8,128)S(1)}, u32[]{:S(2)}, u32[]{:S(2)}) async-start(f32[32,48,128]{2,1,0:T(8,128)} %forecast.1), calls=%async_computation | async-start | bytes 1572864 | tf_op jit(solution)/shard_map/all_to_all | solution.py:320
where the time goes:
time: 145 us; the launch traced here: 144 us
  blocking collectives  59.6 us (41%)
  waiting for transfers between devices  31.1 us (21%)
  starting transfers between devices  24.8 us (17%)
  Pallas kernels  23 us (16%)
  local copies, waits for them, and re-layouts  4.61 us (3%)
    all_to_all x1, blocking collectives, local(): returned = lax.all_to_all(result, MEM, 0, 0, tiled=True)  24.3 us
    all_to_all x1, waiting for transfers between devices, local(): gathered = lax.all_to_all(sent, MEM, 0, 0, tiled=True)  21.4 us
    all_to_all x1, blocking collectives, local(): pieces = lax.all_to_all(total_piece(parts, devices), MEM, 0, 0, tiled=True)  20.8 us
    all_to_all x1, blocking collectives, local(): parts = lax.all_to_all(parts, 'space', 0, 0, tiled=True)  14.6 us
    pallas_call x1, Pallas kernels, forecast(): pl.pallas_call(forecast_kernel, out_shape=jax.ShapeDtypeStruct((blocks, 3...  12.2 us
    pallas_call x1, Pallas kernels, analysis(): pl.pallas_call(analysis_kernel, out_shape=jax.ShapeDtypeStruct((devices,...  10.2 us
    all_to_all x1, starting transfers between devices, local(): gathered = lax.all_to_all(sent, MEM, 0, 0, tiled=True)  10.2 us
    ppermute x1, starting transfers between devices, local(): after = lax.ppermute(planes, 'space', ring('space', -1))  6.13 us
  transfers between devices with their start and end apart: 5, of which 5 were waited for; matrix products, arithmetic and copies ran while one was open for 1% of the time, Pallas kernels for 0%

commit v1 on v0

--- a/solution.py
+++ b/solution.py
@@ -41,14 +41,70 @@
     return pltpu.CompilerParams(vmem_limit_bytes=mebibytes << 20)
 
 
-def forecast_kernel(cells, wide_ref, coriolis_ref, out_ref, a_ref, b_ref, fresh_ref):
-    rows, _, columns = wide_ref.shape
-    members = a_ref.shape[2]
-    rows_here = rows - 2 * HALO
+def planes_kernel(state_hbm, depth_hbm, ocean_hbm, out_ref, state_ref, depth_ref, ocean_ref, sems):
+    members, fields, rows, columns = state_ref.shape
+    copies = [
+        pltpu.make_async_copy(source, target, sems.at[k])
+        for k, (source, target) in enumerate(
+            ((depth_hbm, depth_ref), (ocean_hbm, ocean_ref), (state_hbm, state_ref))
+        )
+    ]
+    for copy in copies:
+        copy.start()
+    copies[0].wait()
+    copies[1].wait()
+    at = fields * members
+    depth = depth_ref[...]
+    ocean = ocean_ref[...].astype(jnp.float32)
+    for r in range(rows):
+        out_ref[r, at : at + 1, :] = depth[r : r + 1]
+        out_ref[r, at + 1 : at + 2, :] = ocean[r : r + 1]
+        out_ref[r, at + 2 : at + 4, :] = jnp.zeros((2, columns), jnp.float32)
+    copies[2].wait()
+    for f in range(fields):
+        for m in range(members):
+            at = f * members + m
+            plane = state_ref[m, f]
+            for r in range(rows):
+                out_ref[r, at : at + 1, :] = plane[r : r + 1]
+
+
+def planes_of(state, depth, ocean):
+    members, fields, rows, columns = state.shape
+    return pl.pallas_call(
+        planes_kernel,
+        out_shape=jax.ShapeDtypeStruct((rows, fields * members + 4, columns), jnp.float32),
+        in_specs=[pl.BlockSpec(memory_space=pltpu.HBM)] * 3,
+        out_specs=pl.BlockSpec(memory_space=pltpu.VMEM),
+        scratch_shapes=[
+            pltpu.VMEM(state.shape, jnp.float32),
+            pltpu.VMEM(depth.shape, jnp.float32),
+            pltpu.VMEM(ocean.shape, jnp.int32),
+            pltpu.SemaphoreType.DMA((3,)),
+        ],
+        compiler_params=room(8),
+        name="planes",
+    )(*(pltpu.with_memory_space_constraint(x, pltpu.HBM) for x in (state, depth, ocean)))
+
+
+def forecast_kernel(
+    places,
+    far_before_ref,
+    before_ref,
+    own_ref,
+    after_ref,
+    far_after_ref,
+    coriolis_ref,
+    out_ref,
+    a_ref,
+    b_ref,
+    fresh_ref,
+    still_ref,
+):
+    _, rows, members, columns = a_ref.shape
+    rows_here = own_ref.shape[0]
     coriolis = coriolis_ref[...] * DT
     parts = [slice(at, min(at + 8, members)) for at in range(0, members, 8)]
-    depth_at = slice(3 * members, 3 * members + 1)
-    ocean_at = slice(3 * members + 1, 3 * members + 2)
 
     def north(x):
         return pltpu.roll(x, columns - 1, 1)
@@ -56,21 +112,26 @@
     def south(x):
         return pltpu.roll(x, 1, 1)
 
-    def unpack(r, carry):
-        for f in range(3):
-            b_ref[f, r] = wide_ref[r, f * members : (f + 1) * members, :]
-        return carry
-
-    lax.fori_loop(0, rows, unpack, 0)
+    at = 0
+    for piece in (far_before_ref, before_ref, own_ref, after_ref, far_after_ref):
+
+        def unpack(r, carry, piece=piece, at=at):
+            for f in range(3):
+                b_ref[f, at + r] = piece[r, f * members : (f + 1) * members, :]
+            still_ref[at + r] = piece[r, 3 * members : 3 * members + 2, :]
+            return carry
+
+        lax.fori_loop(0, piece.shape[0], unpack, 0)
+        at += piece.shape[0]
 
     for step in range(STEPS):
         source, target = (b_ref, a_ref) if step % 2 == 0 else (a_ref, b_ref)
         low = 2 * step
 
         def height_row(r, carry, source=source):
-            depth_above = wide_ref[r + 1, depth_at]
-            depth_below = wide_ref[r - 1, depth_at]
-            depth = wide_ref[r, depth_at]
+            depth_above = still_ref[r + 1, 0:1]
+            depth_below = still_ref[r - 1, 0:1]
+            depth = still_ref[r, 0:1]
             for m in parts:
                 above = (depth_above + source[0, r + 1, m]) * source[1, r + 1, m]
                 below = (depth_below + source[0, r - 1, m]) * source[1, r - 1, m]
@@ -84,7 +145,7 @@
         lax.fori_loop(low + 1, rows - low - 1, height_row, 0)
 
         def flow_row(r, carry, source=source, target=target):
-            ocean = wide_ref[r, ocean_at]
+            ocean = still_ref[r, 1:2]
             for m in parts:
                 u, v = source[1, r, m], source[2, r, m]
                 ue, uw = source[1, r + 1, m], source[1, r - 1, m]
@@ -108,13 +169,9 @@
     lane = lax.broadcasted_iota(jnp.int32, (members, LANES), 1)
 
     def pick(o, found):
-        cell = cells[0, o]
-        row = cell // columns
-        column = cell % columns
-        start = pl.multiple_of((column // LANES) * LANES, LANES)
-        block = source[0, HALO + row, :, pl.ds(start, LANES)]
-        turned = pltpu.roll(block, (o - column % LANES + LANES) % LANES, 1)
-        return jnp.where(lane == o, turned, found)
+        start = pl.multiple_of(places[1, o], LANES)
+        block = source[0, HALO + places[0, o], :, pl.ds(start, LANES)]
+        return jnp.where(lane == o, pltpu.roll(block, places[2, o], 1), found)
 
     picks = lax.fori_loop(0, LANES, pick, jnp.zeros((members, LANES), jnp.float32), unroll=8)
     per_row = columns // LANES
@@ -130,22 +187,24 @@
                 out_ref[d, f * GROUP + members : (f + 1) * GROUP, :] = part
 
 
-def forecast(cells, wide, coriolis, members, blocks):
-    rows, _, columns = wide.shape
+def forecast(places, pieces, coriolis, members, blocks):
+    columns = pieces[0].shape[2]
+    rows = sum(piece.shape[0] for piece in pieces)
     vmem = pl.BlockSpec(memory_space=pltpu.VMEM)
     return pl.pallas_call(
         forecast_kernel,
         out_shape=jax.ShapeDtypeStruct((blocks, 3 * GROUP, LANES), jnp.float32),
-        in_specs=[pl.BlockSpec(memory_space=pltpu.SMEM), vmem, vmem],
+        in_specs=[pl.BlockSpec(memory_space=pltpu.SMEM)] + [vmem] * (len(pieces) + 1),
         out_specs=vmem,
         scratch_shapes=[
             pltpu.VMEM((3, rows, members, columns), jnp.float32),
             pltpu.VMEM((3, rows, members, columns), jnp.float32),
             pltpu.VMEM((rows, members, columns), jnp.float32),
+            pltpu.VMEM((rows, 2, columns), jnp.float32),
         ],
-        compiler_params=room(16),
+        compiler_params=room(20),
         name="forecast",
-    )(cells, wide, coriolis)
+    )(places, *pieces, coriolis)
 
 
 def gram_kernel(own, gathered_ref, value_ref, error_ref, out_ref, picks_ref, stack_ref):
@@ -227,6 +286,7 @@
     ens = 3 * n
     devices = gathered_ref.shape[0]
     members = ens // devices
+    quads = members // 4
     row = lax.broadcasted_iota(jnp.int32, (n, n), 0)
     column = lax.broadcasted_iota(jnp.int32, (n, n), 1)
 
@@ -253,16 +313,18 @@
     identity = jnp.where(same, 1.0, 0.0)
     system = identity + gram_ref[...] * (1.0 / (ens - 1))
     norm_scale = jnp.sqrt(jnp.sum(system * system, keepdims=True))
-    iterate = system / norm_scale
-    inverse = 1.5 * identity - 0.5 * iterate
-    iterate = product(halves(iterate), halves(inverse))
-    for sweep in range(1, NS_ITERS):
-        iterate_halves = halves(iterate)
-        inverse_halves = halves(inverse)
-        factor_halves = halves(1.5 * identity - 0.5 * product(inverse_halves, iterate_halves))
-        inverse = product(inverse_halves, factor_halves)
-        if sweep + 1 < NS_ITERS:
-            iterate = product(iterate_halves, factor_halves)
+    whole = system / norm_scale
+    inverse = None
+    for pair in range(NS_ITERS // 2):
+        whole_halves = halves(whole)
+        square = product(whole_halves, whole_halves)
+        inner = 1.6875 * identity - 0.5625 * whole + 0.0625 * square
+        quartic = product(halves(inner), halves(square)) + (2.25 * identity - 2.4375 * whole)
+        quartic_halves = halves(quartic)
+        inverse = quartic if pair == 0 else product(halves(inverse), quartic_halves)
+        if 2 * pair + 2 < NS_ITERS:
+            growth = product(quartic_halves, quartic_halves)
+            whole = product(whole_halves, halves(growth))
     weights = inverse / jnp.sqrt(norm_scale)
     pulled = jnp.sum(weights * drive, axis=1, keepdims=True)
     mean_weight = jnp.sum(weights * pulled, axis=0, keepdims=True) * (1.0 / (ens - 1))
@@ -279,9 +341,8 @@
         field_ref[f] = center + product(combined, halves(field - center))
     for f in range(3):
         for d in range(devices):
-            out_ref[d, f * members : (f + 1) * members, :] = field_ref[
-                f, d * members : (d + 1) * members, :
-            ]
+            part = field_ref[f, d * members : (d + 1) * members, :]
+            out_ref[d, f * quads : (f + 1) * quads] = part.reshape(quads, 4, n)
 
 
 def analysis(stack, gathered):
@@ -290,7 +351,7 @@
     vmem = pl.BlockSpec(memory_space=pltpu.VMEM)
     return pl.pallas_call(
         analysis_kernel,
-        out_shape=jax.ShapeDtypeStruct((devices, 3 * ens // devices, LANES), jnp.float32),
+        out_shape=jax.ShapeDtypeStruct((devices, 3 * ens // devices // 4, 4, LANES), jnp.float32),
         in_specs=[vmem, vmem],
         out_specs=vmem,
         scratch_shapes=[
@@ -307,18 +368,24 @@
     devices = lax.axis_size(MEM)
     slabs = lax.axis_size("space")
     coriolis = 0.05 + 0.1 * jnp.arange(columns, dtype=jnp.float32)[None] / columns
-    still = jnp.stack([sea_depth, ocean_mask.astype(jnp.float32)], axis=1)
-    moving = ensemble.transpose(2, 1, 0, 3).reshape(rows_here, fields * local_members, columns)
-    planes = jnp.concatenate([moving, still], axis=1)
+    cells = observed_cells[0]
+    places = jnp.stack(
+        [
+            cells // columns,
+            cells % columns // LANES * LANES,
+            (jnp.arange(LANES, dtype=jnp.int32) - cells) % LANES,
+        ]
+    )
+    own = lax.axis_index(MEM).astype(jnp.int32).reshape(1)
+    planes = planes_of(ensemble, sea_depth, ocean_mask)
     edge = HALO - rows_here
     before = lax.ppermute(planes, "space", ring("space", 1))
     after = lax.ppermute(planes, "space", ring("space", -1))
     far_before = lax.ppermute(planes[rows_here - edge :], "space", ring("space", 2))
     far_after = lax.ppermute(planes[:edge], "space", ring("space", -2))
-    wide = jnp.concatenate([far_before, before, planes, after, far_after], axis=0)
-    sent = forecast(observed_cells, wide, coriolis, local_members, devices)
+    pieces = (far_before, before, planes, after, far_after)
+    sent = forecast(places, pieces, coriolis, local_members, devices)
     gathered = lax.all_to_all(sent, MEM, 0, 0, tiled=True)
-    own = lax.axis_index(MEM).astype(jnp.int32).reshape(1)
     parts = gram_piece(own, gathered, observed_values, observed_error, slabs)
     parts = lax.all_to_all(parts, "space", 0, 0, tiled=True)
     pieces = lax.all_to_all(total_piece(parts, devices), MEM, 0, 0, tiled=True)

time: 145 us -> 138 us (0.952)
  local copies, waits for them, and re-layouts: 4.61 us -> 1.2 us
    ppermute x1, starting transfers between devices: 4.28 us -> 1.92 us  [local(): lax.ppermute(planes[rows_here - edge:], 'space', ring('space', 2))]
    ppermute x1, starting transfers between devices: 6.13 us -> 8.49 us  [local(): after = lax.ppermute(planes, 'space', ring('space', -1))]
    ppermute x1, waiting for transfers between devices: 3.14 us -> 1.37 us  [local(): far_after = lax.ppermute(planes[:edge], 'space', ring('space', -2))]
    ppermute x1, waiting for transfers between devices: 4.87 us -> 6.54 us  [local(): lax.ppermute(planes[rows_here - edge:], 'space', ring('space', 2))]
    pallas_call x1, Pallas kernels: 10.2 us -> 8.78 us  [analysis(): pl.pallas_call(analysis_kernel, out_shape=jax.ShapeDtypeStruct((devices,...]
  transfers between devices with their start and end apart: 5 -> 5, of which waited for: 5 -> 3; matrix products, arithmetic and copies ran while one was open for 1% -> 0% of each run, Pallas kernels for 0% -> 0%
where the time goes in v1:
time: 138 us; the launch traced here: 137 us
  blocking collectives  58.7 us (43%)
  waiting for transfers between devices  30 us (22%)
  starting transfers between devices  25.7 us (19%)
  Pallas kernels  21.7 us (16%)
    all_to_all x1, blocking collectives, local(): returned = lax.all_to_all(result, MEM, 0, 0, tiled=True)  23 us
    all_to_all x1, waiting for transfers between devices, local(): gathered = lax.all_to_all(sent, MEM, 0, 0, tiled=True)  22 us
    all_to_all x1, blocking collectives, local(): pieces = lax.all_to_all(total_piece(parts, devices), MEM, 0, 0, tiled=True)  20.8 us
    all_to_all x1, blocking collectives, local(): parts = lax.all_to_all(parts, 'space', 0, 0, tiled=True)  15 us
    pallas_call x1, Pallas kernels, forecast(): pl.pallas_call(forecast_kernel, out_shape=jax.ShapeDtypeStruct((blocks, 3...  11.1 us
    all_to_all x1, starting transfers between devices, local(): gathered = lax.all_to_all(sent, MEM, 0, 0, tiled=True)  10.2 us
    pallas_call x1, Pallas kernels, analysis(): pl.pallas_call(analysis_kernel, out_shape=jax.ShapeDtypeStruct((devices,...  8.78 us
    ppermute x1, starting transfers between devices, local(): after = lax.ppermute(planes, 'space', ring('space', -1))  8.49 us
  transfers between devices with their start and end apart: 5, of which 3 were waited for; matrix products, arithmetic and copies ran while one was open for 0% of the time, Pallas kernels for 0%

profile of v1, /device:TPU:8, one launch (start us, length us, event | category | flops | bytes accessed | tf_op | source)
XLA Modules:
  0.0 137.5 jit_solution(10305911056838186339)
XLA Ops:
  0.0 1.3 planes.1.own_ref
  1.3 0.0 collective-permute-start.1
  1.3 8.5 %collective-permute-start.2 = (f32[4,40,1024]{2,1,0:T(8,128)S(1)}, f32[4,40,1024]{2,1,0:T(8,128)S(1)}, u32[]{:S(2)}, u32[]{:S(2)}) collective-permute-start(f32[4,40,1024]{2,1,0:T(8,128)S(1)} %planes.1.own_ref), channel_id=1, source_target_pairs={{0,15},{1,0},{2,1},{3,2},{4,3},{5,4},{6,5},{7,6},{8,7},{9,8},{10,9... | collective-permute-start | bytes 1966088 | tf_op jit(solution)/shard_map/ppermute | solution.py:383
  9.8 0.1 fusion.2
  9.8 0.0 copy-start.2
  9.9 1.9 %collective-permute-start = (f32[2,40,1024]{2,1,0:T(8,128)S(1)}, f32[2,40,1024]{2,1,0:T(8,128)S(1)}, u32[]{:S(2)}, u32[]{:S(2)}) collective-permute-start(f32[2,40,1024]{2,1,0:T(8,128)S(1)} %get-tuple-element.6), channel_id=1, source_target_pairs={{0,2},{1,3},{2,4},{3,5},{4,6},{5,7},{6,8},{7,9},{8,10},{9,11},{10,... | collective-permute-start | bytes 983048 | tf_op jit(solution)/shard_map/ppermute | solution.py:384
  11.8 5.1 %collective-permute-start.3 = (f32[2,40,1024]{2,1,0:T(8,128)S(1)}, f32[2,40,1024]{2,1,0:T(8,128)S(1)}, u32[]{:S(2)}, u32[]{:S(2)}) collective-permute-start(f32[2,40,1024]{2,1,0:T(8,128)S(1)} %get-tuple-element.5), channel_id=1, source_target_pairs={{0,14},{1,15},{2,0},{3,1},{4,2},{5,3},{6,4},{7,5},{8,6},{9,7},{10,... | collective-permute-start | bytes 983048 | tf_op jit(solution)/shard_map/ppermute | solution.py:385
  17.0 6.5 %collective-permute-done.far_before_ref = f32[2,40,1024]{2,1,0:T(8,128)S(1)} collective-permute-done((f32[2,40,1024]{2,1,0:T(8,128)S(1)}, f32[2,40,1024]{2,1,0:T(8,128)S(1)}, u32[]{:S(2)}, u32[]{:S(2)}) %collective-permute-start) | collective-permute-done | bytes 327712 | tf_op jit(solution)/shard_map/ppermute | solution.py:384
  23.5 1.4 collective-permute-done.3.far_after_ref
  24.9 0.0 collective-permute-done.1.before_ref
  24.9 0.0 collective-permute-done.2.after_ref
  24.9 11.1 %forecast.1 = f32[32,48,128]{2,1,0:T(8,128)} custom-call(s32[3,128]{1,0:T(4,128)S(1)} %pad_add_fusion.places, f32[2,40,1024]{2,1,0:T(8,128)S(1)} %collective-permute-done.far_before_ref, f32[4,40,1024]{2,1,0:T(8,128)S(1)} %collective-permute-done.1.before_ref, f32[4,40,1024]{2,1,0:T(8,128)S(1)} %planes.1.own_ref, ...), custom_call_target="tpu_custom_call" | custom-call | tf_op jit(solution)/shard_map/forecast/pallas_call | solution.py:194
  36.0 10.2 %all-to-all-start = ((f32[32,48,128]{2,1,0:T(8,128)}), f32[32,48,128]{2,1,0:T(8,128)S(1)}, u32[]{:S(2)}, u32[]{:S(2)}) async-start(f32[32,48,128]{2,1,0:T(8,128)} %forecast.1), calls=%async_computation | async-start | bytes 1572864 | tf_op jit(solution)/shard_map/all_to_all | solution.py:388
  46.2 0.0 copy-start
  46.2 0.0 copy-start.1
  46.2 22.0 %all-to-all-done.gathered_ref = f32[32,48,128]{2,1,0:T(8,128)S(1)} async-done(((f32[32,48,128]{2,1,0:T(8,128)}), f32[32,48,128]{2,1,0:T(8,128)S(1)}, u32[]{:S(2)}, u32[]{:S(2)}) %all-to-all-start) | async-done | bytes 786464 | tf_op jit(solution)/shard_map/all_to_all | solution.py:388
  68.3 0.5 gram.1
  68.8 15.0 %all_to_all.20.parts_ref = f32[16,24,128]{2,1,0:T(8,128)S(1)} all-to-all(f32[16,24,128]{2,1,0:T(8,128)S(1)} %gram.1), channel_id=1, replica_groups=mesh['mem_0'=8,'mem_1'=4,'space'=16] {'space'}, dimensions={0} | all-to-all | bytes 393216 | tf_op jit(solution)/shard_map/all_to_all | solution.py:390
  83.8 20.8 %all_to_all.21 = f32[32,24,128]{2,1,0:T(8,128)S(1)} all-to-all(f32[32,24,128]{2,1,0:T(8,128)S(1)} %total.1), channel_id=1, replica_groups=mesh['mem_0'=8,'mem_1'=4,'space'=16] {'mem_0','mem_1'}, dimensions={0} | all-to-all | bytes 786432 | tf_op jit(solution)/shard_map/all_to_all | solution.py:391
  104.6 8.8 %analysis.1 = f32[32,9,4,128]{3,2,1,0:T(4,128)S(1)} custom-call(f32[768,128]{1,0:T(8,128)S(1)} %bitcast.9, f32[32,48,128]{2,1,0:T(8,128)S(1)} %all-to-all-done.gathered_ref), custom_call_target="tpu_custom_call" | custom-call | tf_op jit(solution)/shard_map/analysis/pallas_call | solution.py:352
  113.3 23.0 %all_to_all.22 = f32[32,9,4,128]{3,2,1,0:T(4,128)S(1)} all-to-all(f32[32,9,4,128]{3,2,1,0:T(4,128)S(1)} %analysis.1), channel_id=1, replica_groups=mesh['mem_0'=8,'mem_1'=4,'space'=16] {'mem_0','mem_1'}, dimensions={0} | all-to-all | bytes 1179648 | tf_op jit(solution)/shard_map/all_to_all | solution.py:393
  136.3 0.1 copy.8
  136.4 0.2 reshape.29
  136.6 0.9 copy.9
  (7 shorter events, 0.1 us)
Async XLA Ops:
  1.3 23.6 %collective-permute-start.1 = (f32[4,40,1024]{2,1,0:T(8,128)S(1)}, f32[4,40,1024]{2,1,0:T(8,128)S(1)}, u32[]{:S(2)}, u32[]{:S(2)}) collective-permute-start(f32[4,40,1024]{2,1,0:T(8,128)S(1)} %planes.1.own_ref), channel_id=1, source_target_pairs={{0,1},{1,2},{2,3},{3,4},{4,5},{5,6},{6,7},{7,8},{8,9},{9,10},{10,1... | collective-permute-start | bytes 1966088 | tf_op jit(solution)/shard_map/ppermute | solution.py:382
  1.3 23.6 %collective-permute-start.2 = (f32[4,40,1024]{2,1,0:T(8,128)S(1)}, f32[4,40,1024]{2,1,0:T(8,128)S(1)}, u32[]{:S(2)}, u32[]{:S(2)}) collective-permute-start(f32[4,40,1024]{2,1,0:T(8,128)S(1)} %planes.1.own_ref), channel_id=1, source_target_pairs={{0,15},{1,0},{2,1},{3,2},{4,3},{5,4},{6,5},{7,6},{8,7},{9,8},{10,9... | collective-permute-start | bytes 1966088 | tf_op jit(solution)/shard_map/ppermute | solution.py:383
  9.8 7.1 %copy-start.2 = (s32[1,128]{1,0:T(1,128)S(1)}, s32[1,128]{1,0:T(1,128)}, u32[]{:S(2)}) copy-start(s32[1,128]{1,0:T(1,128)} %param.9) | copy-start | bytes 1540
  9.9 13.7 %collective-permute-start = (f32[2,40,1024]{2,1,0:T(8,128)S(1)}, f32[2,40,1024]{2,1,0:T(8,128)S(1)}, u32[]{:S(2)}, u32[]{:S(2)}) collective-permute-start(f32[2,40,1024]{2,1,0:T(8,128)S(1)} %get-tuple-element.6), channel_id=1, source_target_pairs={{0,2},{1,3},{2,4},{3,5},{4,6},{5,7},{6,8},{7,9},{8,10},{9,11},{10,... | collective-permute-start | bytes 983048 | tf_op jit(solution)/shard_map/ppermute | solution.py:384
  11.8 13.1 %collective-permute-start.3 = (f32[2,40,1024]{2,1,0:T(8,128)S(1)}, f32[2,40,1024]{2,1,0:T(8,128)S(1)}, u32[]{:S(2)}, u32[]{:S(2)}) collective-permute-start(f32[2,40,1024]{2,1,0:T(8,128)S(1)} %get-tuple-element.5), channel_id=1, source_target_pairs={{0,14},{1,15},{2,0},{3,1},{4,2},{5,3},{6,4},{7,5},{8,6},{9,7},{10,... | collective-permute-start | bytes 983048 | tf_op jit(solution)/shard_map/ppermute | solution.py:385
  36.0 32.3 %all-to-all-start = ((f32[32,48,128]{2,1,0:T(8,128)}), f32[32,48,128]{2,1,0:T(8,128)S(1)}, u32[]{:S(2)}, u32[]{:S(2)}) async-start(f32[32,48,128]{2,1,0:T(8,128)} %forecast.1), calls=%async_computation | async-start | bytes 1572864 | tf_op jit(solution)/shard_map/all_to_all | solution.py:388
  46.2 22.1 %copy-start = (f32[1,128]{1,0:T(1,128)S(1)}, f32[1,128]{1,0:T(1,128)}, u32[]{:S(2)}) copy-start(f32[1,128]{1,0:T(1,128)} %value_ref.1) | copy-start | bytes 1540
  46.2 22.1 %copy-start.1 = (f32[1,128]{1,0:T(1,128)S(1)}, f32[1,128]{1,0:T(1,128)}, u32[]{:S(2)}) copy-start(f32[1,128]{1,0:T(1,128)} %error_ref.1) | copy-start | bytes 1540

commit v2 on v1

--- a/solution.py
+++ b/solution.py
@@ -87,85 +87,122 @@
     )(*(pltpu.with_memory_space_constraint(x, pltpu.HBM) for x in (state, depth, ocean)))
 
 
-def forecast_kernel(
+def north(x):
+    return pltpu.roll(x, x.shape[1] - 1, 1)
+
+
+def south(x):
+    return pltpu.roll(x, 1, 1)
+
+
+def sublane_parts(members):
+    return [slice(at, min(at + 8, members)) for at in range(0, members, 8)]
+
+
+def advance(source, target, still, fresh_ref, coriolis, first, last):
+    parts = sublane_parts(source.shape[2])
+
+    def height_row(r, carry):
+        depth_above = still[r + 1, 0:1]
+        depth_below = still[r - 1, 0:1]
+        depth = still[r, 0:1]
+        for m in parts:
+            above = (depth_above + source[0, r + 1, m]) * source[1, r + 1, m]
+            below = (depth_below + source[0, r - 1, m]) * source[1, r - 1, m]
+            height = source[0, r, m]
+            across = (depth + height) * source[2, r, m]
+            fresh_ref[r, m] = height - (0.5 * DT) * (
+                (above - below) + (north(across) - south(across))
+            )
+        return carry
+
+    lax.fori_loop(first - 1, last + 2, height_row, 0)
+
+    def flow_row(r, carry):
+        ocean = still[r, 1:2]
+        for m in parts:
+            u, v = source[1, r, m], source[2, r, m]
+            ue, uw = source[1, r + 1, m], source[1, r - 1, m]
+            un, us = north(u), south(u)
+            tend = GRAV * (fresh_ref[r + 1, m] - fresh_ref[r - 1, m])
+            tend = tend + u * (ue - uw) + v * (un - us)
+            new = (1.0 - 4.0 * DT * VISC) * u - (0.5 * DT) * tend + coriolis * v
+            target[1, r, m] = (new + (DT * VISC) * ((ue + uw) + (un + us))) * ocean
+            fresh = fresh_ref[r, m]
+            target[0, r, m] = fresh
+            ve, vw = source[2, r + 1, m], source[2, r - 1, m]
+            vn, vs = north(v), south(v)
+            tend = GRAV * (north(fresh) - south(fresh)) + u * (ve - vw) + v * (vn - vs)
+            new = (1.0 - 4.0 * DT * VISC) * v - (0.5 * DT) * tend - coriolis * u
+            target[2, r, m] = (new + (DT * VISC) * ((ve + vw) + (vn + vs))) * ocean
+        return carry
+
+    lax.fori_loop(first, last + 1, flow_row, 0)
+
+
+def unpack(piece, count, at, state_ref, still_ref):
+    members = state_ref.shape[2]
+
+    def row(r, carry):
+        for f in range(3):
+            state_ref[f, at + r] = piece[r, f * members : (f + 1) * members, :]
+        still_ref[at + r] = piece[r, 3 * members : 3 * members + 2, :]
+        return carry
+
+    lax.fori_loop(0, count, row, 0)
+
+
+def inner_kernel(
+    before_ref, own_ref, after_ref, coriolis_ref, one_ref, two_ref, raw_ref, a_ref, b_ref,
+    fresh_ref, still_ref,
+):
+    coriolis = coriolis_ref[...] * DT
+    for at, piece in ((2, before_ref), (6, own_ref), (10, after_ref)):
+        unpack(piece, 4, at, raw_ref, still_ref)
+    advance(raw_ref, a_ref, still_ref, fresh_ref, coriolis, 4, 11)
+    advance(a_ref, b_ref, still_ref, fresh_ref, coriolis, 6, 9)
+    for f in range(3):
+        for r in range(8):
+            one_ref[f, r] = a_ref[f, 4 + r]
+        for r in range(4):
+            two_ref[f, r] = b_ref[f, 6 + r]
+
+
+def outer_kernel(
     places,
     far_before_ref,
     before_ref,
     own_ref,
     after_ref,
     far_after_ref,
+    one_ref,
+    two_ref,
     coriolis_ref,
     out_ref,
+    raw_ref,
     a_ref,
     b_ref,
     fresh_ref,
     still_ref,
 ):
-    _, rows, members, columns = a_ref.shape
+    members, columns = raw_ref.shape[2:]
     rows_here = own_ref.shape[0]
     coriolis = coriolis_ref[...] * DT
-    parts = [slice(at, min(at + 8, members)) for at in range(0, members, 8)]
-
-    def north(x):
-        return pltpu.roll(x, columns - 1, 1)
-
-    def south(x):
-        return pltpu.roll(x, 1, 1)
-
-    at = 0
-    for piece in (far_before_ref, before_ref, own_ref, after_ref, far_after_ref):
-
-        def unpack(r, carry, piece=piece, at=at):
-            for f in range(3):
-                b_ref[f, at + r] = piece[r, f * members : (f + 1) * members, :]
-            still_ref[at + r] = piece[r, 3 * members : 3 * members + 2, :]
-            return carry
-
-        lax.fori_loop(0, piece.shape[0], unpack, 0)
-        at += piece.shape[0]
-
-    for step in range(STEPS):
-        source, target = (b_ref, a_ref) if step % 2 == 0 else (a_ref, b_ref)
-        low = 2 * step
-
-        def height_row(r, carry, source=source):
-            depth_above = still_ref[r + 1, 0:1]
-            depth_below = still_ref[r - 1, 0:1]
-            depth = still_ref[r, 0:1]
-            for m in parts:
-                above = (depth_above + source[0, r + 1, m]) * source[1, r + 1, m]
-                below = (depth_below + source[0, r - 1, m]) * source[1, r - 1, m]
-                height = source[0, r, m]
-                across = (depth + height) * source[2, r, m]
-                fresh_ref[r, m] = height - (0.5 * DT) * (
-                    (above - below) + (north(across) - south(across))
-                )
-            return carry
-
-        lax.fori_loop(low + 1, rows - low - 1, height_row, 0)
-
-        def flow_row(r, carry, source=source, target=target):
-            ocean = still_ref[r, 1:2]
-            for m in parts:
-                u, v = source[1, r, m], source[2, r, m]
-                ue, uw = source[1, r + 1, m], source[1, r - 1, m]
-                un, us = north(u), south(u)
-                tend = GRAV * (fresh_ref[r + 1, m] - fresh_ref[r - 1, m])
-                tend = tend + u * (ue - uw) + v * (un - us)
-                new = (1.0 - 4.0 * DT * VISC) * u - (0.5 * DT) * tend + coriolis * v
-                target[1, r, m] = (new + (DT * VISC) * ((ue + uw) + (un + us))) * ocean
-                fresh = fresh_ref[r, m]
-                target[0, r, m] = fresh
-                ve, vw = source[2, r + 1, m], source[2, r - 1, m]
-                vn, vs = north(v), south(v)
-                tend = GRAV * (north(fresh) - south(fresh)) + u * (ve - vw) + v * (vn - vs)
-                new = (1.0 - 4.0 * DT * VISC) * v - (0.5 * DT) * tend - coriolis * u
-                target[2, r, m] = (new + (DT * VISC) * ((ve + vw) + (vn + vs))) * ocean
-            return carry
-
-        lax.fori_loop(low + 2, rows - low - 2, flow_row, 0)
-    source = target
-
+    for at, piece in ((0, far_before_ref), (2, before_ref), (10, after_ref), (14, far_after_ref)):
+        unpack(piece, piece.shape[0], at, raw_ref, still_ref)
+    for r in range(rows_here):
+        still_ref[6 + r] = own_ref[r, 3 * members : 3 * members + 2, :]
+    for f in range(3):
+        for r in range(8):
+            a_ref[f, 4 + r] = one_ref[f, r]
+        for r in range(4):
+            b_ref[f, 6 + r] = two_ref[f, r]
+    advance(raw_ref, a_ref, still_ref, fresh_ref, coriolis, 2, 3)
+    advance(raw_ref, a_ref, still_ref, fresh_ref, coriolis, 12, 13)
+    advance(a_ref, b_ref, still_ref, fresh_ref, coriolis, 4, 5)
+    advance(a_ref, b_ref, still_ref, fresh_ref, coriolis, 10, 11)
+    advance(b_ref, raw_ref, still_ref, fresh_ref, coriolis, 6, 9)
+    source = raw_ref
     lane = lax.broadcasted_iota(jnp.int32, (members, LANES), 1)
 
     def pick(o, found):
@@ -187,24 +224,42 @@
                 out_ref[d, f * GROUP + members : (f + 1) * GROUP, :] = part
 
 
-def forecast(places, pieces, coriolis, members, blocks):
+def frame(members, columns):
+    rows = 2 * HALO + 4
+    return [pltpu.VMEM((3, rows, members, columns), jnp.float32)] * 3 + [
+        pltpu.VMEM((rows, members, columns), jnp.float32),
+        pltpu.VMEM((rows, 2, columns), jnp.float32),
+    ]
+
+
+def inner_rows(near, coriolis, members):
+    columns = near[0].shape[2]
+    vmem = pl.BlockSpec(memory_space=pltpu.VMEM)
+    return pl.pallas_call(
+        inner_kernel,
+        out_shape=tuple(
+            jax.ShapeDtypeStruct((3, rows, members, columns), jnp.float32) for rows in (8, 4)
+        ),
+        in_specs=[vmem] * 4,
+        out_specs=(vmem, vmem),
+        scratch_shapes=frame(members, columns),
+        compiler_params=room(20),
+        name="inner",
+    )(*near, coriolis)
+
+
+def forecast(places, pieces, inner, coriolis, members, blocks):
     columns = pieces[0].shape[2]
-    rows = sum(piece.shape[0] for piece in pieces)
     vmem = pl.BlockSpec(memory_space=pltpu.VMEM)
     return pl.pallas_call(
-        forecast_kernel,
+        outer_kernel,
         out_shape=jax.ShapeDtypeStruct((blocks, 3 * GROUP, LANES), jnp.float32),
-        in_specs=[pl.BlockSpec(memory_space=pltpu.SMEM)] + [vmem] * (len(pieces) + 1),
+        in_specs=[pl.BlockSpec(memory_space=pltpu.SMEM)] + [vmem] * 8,
         out_specs=vmem,
-        scratch_shapes=[
-            pltpu.VMEM((3, rows, members, columns), jnp.float32),
-            pltpu.VMEM((3, rows, members, columns), jnp.float32),
-            pltpu.VMEM((rows, members, columns), jnp.float32),
-            pltpu.VMEM((rows, 2, columns), jnp.float32),
-        ],
+        scratch_shapes=frame(members, columns),
         compiler_params=room(20),
-        name="forecast",
-    )(places, *pieces, coriolis)
+        name="outer",
+    )(places, *pieces, *inner, coriolis)
 
 
 def gram_kernel(own, gathered_ref, value_ref, error_ref, out_ref, picks_ref, stack_ref):
@@ -230,34 +285,43 @@
     row = lax.broadcasted_iota(jnp.int32, (n, n), 0)
     column = lax.broadcasted_iota(jnp.int32, (n, n), 1)
     middle = gram[n : 2 * n, n : 2 * n]
-    stack_ref[0:n] = gram[0:n, n : 2 * n]
-    stack_ref[n : 2 * n] = gram[0:n, 2 * n :]
-    stack_ref[2 * n : 3 * n] = gram[n : 2 * n, 2 * n :]
-    stack_ref[3 * n : 4 * n] = jnp.where(row <= column, gram[0:n, 0:n], middle)
-    stack_ref[4 * n : 5 * n] = gram[2 * n :, 2 * n :]
-    stack_ref[5 * n :] = jnp.zeros((n, n), jnp.float32)
     diagonal = jnp.sum(jnp.where(row == column, middle, 0.0), axis=0, keepdims=True)
-    stack_ref[5 * n : 5 * n + 1] = diagonal
-    for k in range(3):
-        stack_ref[5 * n + 8 * (k + 1) : 5 * n + 8 * (k + 2)] = drive[:, k * n : (k + 1) * n]
+    last = gram[2 * n :, 2 * n :]
+    vectors = [jnp.broadcast_to(diagonal, (8, n))]
+    vectors += [drive[:, k * n : (k + 1) * n] for k in range(3)]
+    for k, vector in enumerate(vectors):
+        turned = pltpu.roll(vector, n // 2, 1)
+        left = column < n // 2
+        last = jnp.where((row == n - 8 + 2 * k) & left, vector[0:1], last)
+        last = jnp.where((row == n - 7 + 2 * k) & left, turned[0:1], last)
+    blocks = (
+        gram[0:n, n : 2 * n],
+        gram[0:n, 2 * n :],
+        gram[n : 2 * n, 2 * n :],
+        jnp.where(row <= column, gram[0:n, 0:n], middle),
+        last,
+    )
+    quads = n // 4
+    for k, block in enumerate(blocks):
+        stack_ref[k * quads : (k + 1) * quads] = block.reshape(quads, 4, n)
     size = out_ref.shape[1]
-    piece = stack_ref[pl.ds(pl.multiple_of(own[0] * size, 8), size), :]
+    piece = stack_ref[pl.ds(own[0] * size, size)]
     out_ref[...] = jnp.broadcast_to(piece[None], out_ref.shape)
 
 
 def gram_piece(own, gathered, value, error, slabs):
     devices = gathered.shape[0]
     ens = 3 * LANES
-    size = 6 * LANES // devices
+    size = 5 * LANES // 4 // devices
     vmem = pl.BlockSpec(memory_space=pltpu.VMEM)
     return pl.pallas_call(
         gram_kernel,
-        out_shape=jax.ShapeDtypeStruct((slabs, size, LANES), jnp.float32),
+        out_shape=jax.ShapeDtypeStruct((slabs, size, 4, LANES), jnp.float32),
         in_specs=[pl.BlockSpec(memory_space=pltpu.SMEM), vmem, vmem, vmem],
         out_specs=vmem,
         scratch_shapes=[
             pltpu.VMEM((ens, LANES), jnp.float32),
-            pltpu.VMEM((6 * LANES, LANES), jnp.float32),
+            pltpu.VMEM((5 * LANES // 4, 4, LANES), jnp.float32),
         ],
         compiler_params=room(8),
         name="gram",
@@ -291,7 +355,7 @@
     column = lax.broadcasted_iota(jnp.int32, (n, n), 1)
 
     def block(k):
-        return stack_ref[k * n : (k + 1) * n]
+        return stack_ref[k * n // 4 : (k + 1) * n // 4].reshape(n, n)
 
     for k, (i, j) in enumerate(((0, 1), (0, 2), (1, 2))):
         gram_ref[i * n : (i + 1) * n, j * n : (j + 1) * n] = block(k)
@@ -300,12 +364,18 @@
     upper = jnp.where(row < column, both, 0.0)
     gram_ref[0:n, 0:n] = upper + upper.T + jnp.where(row == column, both, 0.0)
     lower = jnp.where(row > column, both, 0.0)
-    middle = jnp.where(row == column, stack_ref[5 * n : 5 * n + 1], 0.0)
+    last = block(4)
+    tail = last[n - 8 :]
+    turned = pltpu.roll(tail, n // 2, 1)
+    left = column[0:1] < n // 2
+    vectors = [
+        jnp.where(left, tail[2 * k : 2 * k + 1], turned[2 * k + 1 : 2 * k + 2]) for k in range(4)
+    ]
+    middle = jnp.where(row == column, vectors[0], 0.0)
     gram_ref[n : 2 * n, n : 2 * n] = lower + lower.T + middle
-    gram_ref[2 * n :, 2 * n :] = block(4)
-    drive = jnp.concatenate(
-        [stack_ref[5 * n + 8 * (k + 1) : 5 * n + 8 * (k + 1) + 1] for k in range(3)], axis=1
-    )
+    upper = jnp.where(row < column, last, 0.0)
+    gram_ref[2 * n :, 2 * n :] = upper + upper.T + jnp.where(row == column, last, 0.0)
+    drive = jnp.concatenate(vectors[1:], axis=1)
 
     same = lax.broadcasted_iota(jnp.int32, (ens, ens), 0) == lax.broadcasted_iota(
         jnp.int32, (ens, ens), 1
@@ -383,13 +453,14 @@
     after = lax.ppermute(planes, "space", ring("space", -1))
     far_before = lax.ppermute(planes[rows_here - edge :], "space", ring("space", 2))
     far_after = lax.ppermute(planes[:edge], "space", ring("space", -2))
+    inner = inner_rows((before, planes, after), coriolis, local_members)
     pieces = (far_before, before, planes, after, far_after)
-    sent = forecast(places, pieces, coriolis, local_members, devices)
+    sent = forecast(places, pieces, inner, coriolis, local_members, devices)
     gathered = lax.all_to_all(sent, MEM, 0, 0, tiled=True)
     parts = gram_piece(own, gathered, observed_values, observed_error, slabs)
     parts = lax.all_to_all(parts, "space", 0, 0, tiled=True)
     pieces = lax.all_to_all(total_piece(parts, devices), MEM, 0, 0, tiled=True)
-    result = analysis(pieces.reshape(-1, LANES), gathered)
+    result = analysis(pieces.reshape(-1, 4, LANES), gathered)
     returned = lax.all_to_all(result, MEM, 0, 0, tiled=True)
     returned = returned.reshape(rows_here, columns // LANES, fields, local_members, LANES)
     return returned.transpose(3, 2, 0, 1, 4).reshape(ensemble.shape)

time: 138 us -> 134 us (0.971)
  waiting for transfers between devices: 30 us -> 26.1 us
  Pallas kernels: 21.7 us -> 23.1 us
    ppermute x1, waiting for transfers between devices: 6.54 us -> 0.01 us  [local(): lax.ppermute(planes[rows_here - edge:], 'space', ring('space', 2))]
    ppermute x1, waiting for transfers between devices: 0.01 us -> 2.55 us  [local(): before = lax.ppermute(planes, 'space', ring('space', 1))]
    ppermute x1, waiting for transfers between devices: 0.01 us -> 1.38 us  [local(): after = lax.ppermute(planes, 'space', ring('space', -1))]
    pallas_call x1 -> x2, Pallas kernels: 11.1 us -> 12.5 us  [the longest x1 8.1 us: forecast(): pl.pallas_call(outer_kernel, out_shape=jax.ShapeDtypeStruct((blocks, 3 *...]
  transfers between devices with their start and end apart: 5 -> 5, of which waited for: 3 -> 3; matrix products, arithmetic and copies ran while one was open for 0% -> 0% of each run, Pallas kernels for 0% -> 3%
where the time goes in v2:
time: 134 us
  blocking collectives  57.6 us (43%)
  waiting for transfers between devices  26.1 us (19%)
  starting transfers between devices  25.9 us (19%)
  Pallas kernels  23.1 us (17%)
    all_to_all x1, blocking collectives, local(): returned = lax.all_to_all(result, MEM, 0, 0, tiled=True)  22.6 us
    all_to_all x1, waiting for transfers between devices, local(): gathered = lax.all_to_all(sent, MEM, 0, 0, tiled=True)  22.2 us
    all_to_all x1, blocking collectives, local(): pieces = lax.all_to_all(total_piece(parts, devices), MEM, 0, 0, tiled=True)  20.4 us
    all_to_all x1, blocking collectives, local(): parts = lax.all_to_all(parts, 'space', 0, 0, tiled=True)  14.6 us
    all_to_all x1, starting transfers between devices, local(): gathered = lax.all_to_all(sent, MEM, 0, 0, tiled=True)  10.3 us
    pallas_call x1, Pallas kernels, analysis(): pl.pallas_call(analysis_kernel, out_shape=jax.ShapeDtypeStruct((devices,...  8.77 us
    ppermute x1, starting transfers between devices, local(): after = lax.ppermute(planes, 'space', ring('space', -1))  8.49 us
    pallas_call x1, Pallas kernels, forecast(): pl.pallas_call(outer_kernel, out_shape=jax.ShapeDtypeStruct((blocks, 3 *...  8.1 us
  transfers between devices with their start and end apart: 5, of which 3 were waited for; matrix products, arithmetic and copies ran while one was open for 0% of the time, Pallas kernels for 3%

profile of v2, /device:TPU:8, one launch (start us, length us, event | category | flops | bytes accessed | tf_op | source)
XLA Modules:
  0.0 134.1 jit_solution(9407681110777972208)
XLA Ops:
  0.0 1.3 planes.1.own_ref
  1.3 0.0 collective-permute-start.1
  1.3 8.5 %collective-permute-start.2 = (f32[4,40,1024]{2,1,0:T(8,128)S(1)}, f32[4,40,1024]{2,1,0:T(8,128)S(1)}, u32[]{:S(2)}, u32[]{:S(2)}) collective-permute-start(f32[4,40,1024]{2,1,0:T(8,128)S(1)} %planes.1.own_ref), channel_id=1, source_target_pairs={{0,15},{1,0},{2,1},{3,2},{4,3},{5,4},{6,5},{7,6},{8,7},{9,8},{10,9... | collective-permute-start | bytes 1966088 | tf_op jit(solution)/shard_map/ppermute | solution.py:453
  9.8 0.1 fusion.2
  9.9 1.9 %collective-permute-start = (f32[2,40,1024]{2,1,0:T(8,128)S(1)}, f32[2,40,1024]{2,1,0:T(8,128)S(1)}, u32[]{:S(2)}, u32[]{:S(2)}) collective-permute-start(f32[2,40,1024]{2,1,0:T(8,128)S(1)} %get-tuple-element.10), channel_id=1, source_target_pairs={{0,2},{1,3},{2,4},{3,5},{4,6},{5,7},{6,8},{7,9},{8,10},{9,11},{10,... | collective-permute-start | bytes 983048 | tf_op jit(solution)/shard_map/ppermute | solution.py:454
  11.8 5.1 %collective-permute-start.3 = (f32[2,40,1024]{2,1,0:T(8,128)S(1)}, f32[2,40,1024]{2,1,0:T(8,128)S(1)}, u32[]{:S(2)}, u32[]{:S(2)}) collective-permute-start(f32[2,40,1024]{2,1,0:T(8,128)S(1)} %get-tuple-element.9), channel_id=1, source_target_pairs={{0,14},{1,15},{2,0},{3,1},{4,2},{5,3},{6,4},{7,5},{8,6},{9,7},{10,... | collective-permute-start | bytes 983048 | tf_op jit(solution)/shard_map/ppermute | solution.py:455
  16.9 0.0 copy-done.2
  17.0 2.5 %collective-permute-done.1.before_ref = f32[4,40,1024]{2,1,0:T(8,128)S(1)} collective-permute-done((f32[4,40,1024]{2,1,0:T(8,128)S(1)}, f32[4,40,1024]{2,1,0:T(8,128)S(1)}, u32[]{:S(2)}, u32[]{:S(2)}) %collective-permute-start.1) | collective-permute-done | bytes 655392 | tf_op jit(solution)/shard_map/ppermute | solution.py:452
  19.6 1.4 %collective-permute-done.2.after_ref = f32[4,40,1024]{2,1,0:T(8,128)S(1)} collective-permute-done((f32[4,40,1024]{2,1,0:T(8,128)S(1)}, f32[4,40,1024]{2,1,0:T(8,128)S(1)}, u32[]{:S(2)}, u32[]{:S(2)}) %collective-permute-start.2) | collective-permute-done | bytes 655392 | tf_op jit(solution)/shard_map/ppermute | solution.py:453
  20.9 4.4 %inner.1 = (f32[3,8,12,1024]{3,2,1,0:T(8,128)S(1)}, f32[3,4,12,1024]{3,2,1,0:T(8,128)S(1)}) custom-call(f32[4,40,1024]{2,1,0:T(8,128)S(1)} %collective-permute-done.1.before_ref, f32[4,40,1024]{2,1,0:T(8,128)S(1)} %planes.1.own_ref, f32[4,40,1024]{2,1,0:T(8,128)S(1)} %collective-permute-done.2.after_ref, f32[1,1024]{1,0:T(1,128)S(1)} %multiply_add_fusion.coriolis_ref), custom_call_target="tpu_custom_call" | custom-call | tf_op jit(solution)/shard_map/inner/pallas_call | solution.py:238
  25.3 0.0 collective-permute-done.far_before_ref
  25.3 0.0 collective-permute-done.3.far_after_ref
  25.3 8.1 %outer.1 = f32[32,48,128]{2,1,0:T(8,128)} custom-call(s32[3,128]{1,0:T(4,128)S(1)} %pad_add_fusion.places, f32[2,40,1024]{2,1,0:T(8,128)S(1)} %collective-permute-done.far_before_ref, f32[4,40,1024]{2,1,0:T(8,128)S(1)} %collective-permute-done.1.before_ref, f32[4,40,1024]{2,1,0:T(8,128)S(1)} %planes.1.own_ref, ...), custom_call_target="tpu_custom_call" | custom-call | tf_op jit(solution)/shard_map/outer/pallas_call | solution.py:254
  33.4 10.3 %all-to-all-start = ((f32[32,48,128]{2,1,0:T(8,128)}), f32[32,48,128]{2,1,0:T(8,128)S(1)}, u32[]{:S(2)}, u32[]{:S(2)}) async-start(f32[32,48,128]{2,1,0:T(8,128)} %outer.1), calls=%async_computation | async-start | bytes 1572864 | tf_op jit(solution)/shard_map/all_to_all | solution.py:459
  43.7 22.2 %all-to-all-done.gathered_ref = f32[32,48,128]{2,1,0:T(8,128)S(1)} async-done(((f32[32,48,128]{2,1,0:T(8,128)}), f32[32,48,128]{2,1,0:T(8,128)S(1)}, u32[]{:S(2)}, u32[]{:S(2)}) %all-to-all-start) | async-done | bytes 786464 | tf_op jit(solution)/shard_map/all_to_all | solution.py:459
  65.9 0.6 gram.1
  66.5 14.6 %all_to_all.20.parts_ref = f32[16,5,4,128]{3,2,1,0:T(4,128)S(1)} all-to-all(f32[16,5,4,128]{3,2,1,0:T(4,128)S(1)} %gram.1), channel_id=1, replica_groups=mesh['mem_0'=8,'mem_1'=4,'space'=16] {'space'}, dimensions={0} | all-to-all | bytes 327680 | tf_op jit(solution)/shard_map/all_to_all | solution.py:461
  81.1 0.1 total.1
  81.2 20.4 %all_to_all.21 = f32[32,5,4,128]{3,2,1,0:T(4,128)S(1)} all-to-all(f32[32,5,4,128]{3,2,1,0:T(4,128)S(1)} %total.1), channel_id=1, replica_groups=mesh['mem_0'=8,'mem_1'=4,'space'=16] {'mem_0','mem_1'}, dimensions={0} | all-to-all | bytes 655360 | tf_op jit(solution)/shard_map/all_to_all | solution.py:462
  101.6 8.8 %analysis.1 = f32[32,9,4,128]{3,2,1,0:T(4,128)S(1)} custom-call(f32[160,4,128]{2,1,0:T(4,128)S(1)} %bitcast.9, f32[32,48,128]{2,1,0:T(8,128)S(1)} %all-to-all-done.gathered_ref), custom_call_target="tpu_custom_call" | custom-call | tf_op jit(solution)/shard_map/analysis/pallas_call | solution.py:422
  110.3 22.6 %all_to_all.22 = f32[32,9,4,128]{3,2,1,0:T(4,128)S(1)} all-to-all(f32[32,9,4,128]{3,2,1,0:T(4,128)S(1)} %analysis.1), channel_id=1, replica_groups=mesh['mem_0'=8,'mem_1'=4,'space'=16] {'mem_0','mem_1'}, dimensions={0} | all-to-all | bytes 1179648 | tf_op jit(solution)/shard_map/all_to_all | solution.py:464
  132.9 0.1 copy.8
  133.0 0.2 reshape.29
  133.2 0.9 copy.9
  (8 shorter events, 0.1 us)
Async XLA Ops:
  0.0 16.9 %copy-start.2 = (s32[1,128]{1,0:T(1,128)S(1)}, s32[1,128]{1,0:T(1,128)}, u32[]{:S(2)}) copy-start(s32[1,128]{1,0:T(1,128)} %param.9) | copy-start | bytes 1540
  1.3 18.3 %collective-permute-start.1 = (f32[4,40,1024]{2,1,0:T(8,128)S(1)}, f32[4,40,1024]{2,1,0:T(8,128)S(1)}, u32[]{:S(2)}, u32[]{:S(2)}) collective-permute-start(f32[4,40,1024]{2,1,0:T(8,128)S(1)} %planes.1.own_ref), channel_id=1, source_target_pairs={{0,1},{1,2},{2,3},{3,4},{4,5},{5,6},{6,7},{7,8},{8,9},{9,10},{10,1... | collective-permute-start | bytes 1966088 | tf_op jit(solution)/shard_map/ppermute | solution.py:452
  1.3 19.6 %collective-permute-start.2 = (f32[4,40,1024]{2,1,0:T(8,128)S(1)}, f32[4,40,1024]{2,1,0:T(8,128)S(1)}, u32[]{:S(2)}, u32[]{:S(2)}) collective-permute-start(f32[4,40,1024]{2,1,0:T(8,128)S(1)} %planes.1.own_ref), channel_id=1, source_target_pairs={{0,15},{1,0},{2,1},{3,2},{4,3},{5,4},{6,5},{7,6},{8,7},{9,8},{10,9... | collective-permute-start | bytes 1966088 | tf_op jit(solution)/shard_map/ppermute | solution.py:453
  9.9 15.4 %collective-permute-start = (f32[2,40,1024]{2,1,0:T(8,128)S(1)}, f32[2,40,1024]{2,1,0:T(8,128)S(1)}, u32[]{:S(2)}, u32[]{:S(2)}) collective-permute-start(f32[2,40,1024]{2,1,0:T(8,128)S(1)} %get-tuple-element.10), channel_id=1, source_target_pairs={{0,2},{1,3},{2,4},{3,5},{4,6},{5,7},{6,8},{7,9},{8,10},{9,11},{10,... | collective-permute-start | bytes 983048 | tf_op jit(solution)/shard_map/ppermute | solution.py:454
  11.8 13.5 %collective-permute-start.3 = (f32[2,40,1024]{2,1,0:T(8,128)S(1)}, f32[2,40,1024]{2,1,0:T(8,128)S(1)}, u32[]{:S(2)}, u32[]{:S(2)}) collective-permute-start(f32[2,40,1024]{2,1,0:T(8,128)S(1)} %get-tuple-element.9), channel_id=1, source_target_pairs={{0,14},{1,15},{2,0},{3,1},{4,2},{5,3},{6,4},{7,5},{8,6},{9,7},{10,... | collective-permute-start | bytes 983048 | tf_op jit(solution)/shard_map/ppermute | solution.py:455
  33.4 32.5 %copy-start = (f32[1,128]{1,0:T(1,128)S(1)}, f32[1,128]{1,0:T(1,128)}, u32[]{:S(2)}) copy-start(f32[1,128]{1,0:T(1,128)} %value_ref.1) | copy-start | bytes 1540
  33.4 32.5 %copy-start.1 = (f32[1,128]{1,0:T(1,128)S(1)}, f32[1,128]{1,0:T(1,128)}, u32[]{:S(2)}) copy-start(f32[1,128]{1,0:T(1,128)} %error_ref.1) | copy-start | bytes 1540
  33.4 32.5 %all-to-all-start = ((f32[32,48,128]{2,1,0:T(8,128)}), f32[32,48,128]{2,1,0:T(8,128)S(1)}, u32[]{:S(2)}, u32[]{:S(2)}) async-start(f32[32,48,128]{2,1,0:T(8,128)} %outer.1), calls=%async_computation | async-start | bytes 1572864 | tf_op jit(solution)/shard_map/all_to_all | solution.py:459

commit v3 on v2

--- a/solution.py
+++ b/solution.py
@@ -99,30 +99,47 @@
     return [slice(at, min(at + 8, members)) for at in range(0, members, 8)]
 
 
-def advance(source, target, still, fresh_ref, coriolis, first, last):
-    parts = sublane_parts(source.shape[2])
+def repeat(first, last, row, unroll):
+    if unroll:
+        for r in range(first, last):
+            row(r, 0)
+    else:
+        lax.fori_loop(first, last, row, 0)
+
+
+def rows_of(ref, inner=None, first=0, last=-1):
+    def get(f, r, m):
+        return (inner if inner is not None and first <= r <= last else ref)[f, r, m]
+
+    return get
+
+
+def advance(get, target, still, fresh_ref, coriolis, first, last, known=None, unroll=False):
+    parts = sublane_parts(target.shape[2])
 
     def height_row(r, carry):
         depth_above = still[r + 1, 0:1]
         depth_below = still[r - 1, 0:1]
         depth = still[r, 0:1]
         for m in parts:
-            above = (depth_above + source[0, r + 1, m]) * source[1, r + 1, m]
-            below = (depth_below + source[0, r - 1, m]) * source[1, r - 1, m]
-            height = source[0, r, m]
-            across = (depth + height) * source[2, r, m]
+            above = (depth_above + get(0, r + 1, m)) * get(1, r + 1, m)
+            below = (depth_below + get(0, r - 1, m)) * get(1, r - 1, m)
+            height = get(0, r, m)
+            across = (depth + height) * get(2, r, m)
             fresh_ref[r, m] = height - (0.5 * DT) * (
                 (above - below) + (north(across) - south(across))
             )
         return carry
 
-    lax.fori_loop(first - 1, last + 2, height_row, 0)
+    low = first if known == first - 1 else first - 1
+    high = last if known == last + 1 else last + 1
+    repeat(low, high + 1, height_row, unroll)
 
     def flow_row(r, carry):
         ocean = still[r, 1:2]
         for m in parts:
-            u, v = source[1, r, m], source[2, r, m]
-            ue, uw = source[1, r + 1, m], source[1, r - 1, m]
+            u, v = get(1, r, m), get(2, r, m)
+            ue, uw = get(1, r + 1, m), get(1, r - 1, m)
             un, us = north(u), south(u)
             tend = GRAV * (fresh_ref[r + 1, m] - fresh_ref[r - 1, m])
             tend = tend + u * (ue - uw) + v * (un - us)
@@ -130,14 +147,14 @@
             target[1, r, m] = (new + (DT * VISC) * ((ue + uw) + (un + us))) * ocean
             fresh = fresh_ref[r, m]
             target[0, r, m] = fresh
-            ve, vw = source[2, r + 1, m], source[2, r - 1, m]
+            ve, vw = get(2, r + 1, m), get(2, r - 1, m)
             vn, vs = north(v), south(v)
             tend = GRAV * (north(fresh) - south(fresh)) + u * (ve - vw) + v * (vn - vs)
             new = (1.0 - 4.0 * DT * VISC) * v - (0.5 * DT) * tend - coriolis * u
             target[2, r, m] = (new + (DT * VISC) * ((ve + vw) + (vn + vs))) * ocean
         return carry
 
-    lax.fori_loop(first, last + 1, flow_row, 0)
+    repeat(first, last + 1, flow_row, unroll)
 
 
 def unpack(piece, count, at, state_ref, still_ref):
@@ -153,19 +170,13 @@
 
 
 def inner_kernel(
-    before_ref, own_ref, after_ref, coriolis_ref, one_ref, two_ref, raw_ref, a_ref, b_ref,
-    fresh_ref, still_ref,
+    before_ref, own_ref, after_ref, coriolis_ref, a_ref, b_ref, raw_ref, fresh_ref, still_ref
 ):
     coriolis = coriolis_ref[...] * DT
     for at, piece in ((2, before_ref), (6, own_ref), (10, after_ref)):
         unpack(piece, 4, at, raw_ref, still_ref)
-    advance(raw_ref, a_ref, still_ref, fresh_ref, coriolis, 4, 11)
-    advance(a_ref, b_ref, still_ref, fresh_ref, coriolis, 6, 9)
-    for f in range(3):
-        for r in range(8):
-            one_ref[f, r] = a_ref[f, 4 + r]
-        for r in range(4):
-            two_ref[f, r] = b_ref[f, 6 + r]
+    advance(rows_of(raw_ref), a_ref, still_ref, fresh_ref, coriolis, 4, 11)
+    advance(rows_of(a_ref), b_ref, still_ref, fresh_ref, coriolis, 6, 9)
 
 
 def outer_kernel(
@@ -179,9 +190,9 @@
     two_ref,
     coriolis_ref,
     out_ref,
-    raw_ref,
     a_ref,
     b_ref,
+    raw_ref,
     fresh_ref,
     still_ref,
 ):
@@ -192,16 +203,18 @@
         unpack(piece, piece.shape[0], at, raw_ref, still_ref)
     for r in range(rows_here):
         still_ref[6 + r] = own_ref[r, 3 * members : 3 * members + 2, :]
-    for f in range(3):
-        for r in range(8):
-            a_ref[f, 4 + r] = one_ref[f, r]
-        for r in range(4):
-            b_ref[f, 6 + r] = two_ref[f, r]
-    advance(raw_ref, a_ref, still_ref, fresh_ref, coriolis, 2, 3)
-    advance(raw_ref, a_ref, still_ref, fresh_ref, coriolis, 12, 13)
-    advance(a_ref, b_ref, still_ref, fresh_ref, coriolis, 4, 5)
-    advance(a_ref, b_ref, still_ref, fresh_ref, coriolis, 10, 11)
-    advance(b_ref, raw_ref, still_ref, fresh_ref, coriolis, 6, 9)
+    raw = rows_of(raw_ref)
+    one = rows_of(a_ref, one_ref, 4, 11)
+    two = rows_of(b_ref, two_ref, 6, 9)
+    for r in (4, 11):
+        fresh_ref[r] = one_ref[0, r]
+    advance(raw, a_ref, still_ref, fresh_ref, coriolis, 2, 3, 4, True)
+    advance(raw, a_ref, still_ref, fresh_ref, coriolis, 12, 13, 11, True)
+    for r in (6, 9):
+        fresh_ref[r] = two_ref[0, r]
+    advance(one, b_ref, still_ref, fresh_ref, coriolis, 4, 5, 6, True)
+    advance(one, b_ref, still_ref, fresh_ref, coriolis, 10, 11, 9, True)
+    advance(two, raw_ref, still_ref, fresh_ref, coriolis, 6, 9, None, True)
     source = raw_ref
     lane = lax.broadcasted_iota(jnp.int32, (members, LANES), 1)
 
@@ -226,7 +239,8 @@
 
 def frame(members, columns):
     rows = 2 * HALO + 4
-    return [pltpu.VMEM((3, rows, members, columns), jnp.float32)] * 3 + [
+    return [
+        pltpu.VMEM((3, rows, members, columns), jnp.float32),
         pltpu.VMEM((rows, members, columns), jnp.float32),
         pltpu.VMEM((rows, 2, columns), jnp.float32),
     ]
@@ -237,9 +251,9 @@
     vmem = pl.BlockSpec(memory_space=pltpu.VMEM)
     return pl.pallas_call(
         inner_kernel,
-        out_shape=tuple(
-            jax.ShapeDtypeStruct((3, rows, members, columns), jnp.float32) for rows in (8, 4)
-        ),
+        out_shape=(
+            jax.ShapeDtypeStruct((3, 2 * HALO + 4, members, columns), jnp.float32),
+        ) * 2,
         in_specs=[vmem] * 4,
         out_specs=(vmem, vmem),
         scratch_shapes=frame(members, columns),
@@ -256,7 +270,7 @@
         out_shape=jax.ShapeDtypeStruct((blocks, 3 * GROUP, LANES), jnp.float32),
         in_specs=[pl.BlockSpec(memory_space=pltpu.SMEM)] + [vmem] * 8,
         out_specs=vmem,
-        scratch_shapes=frame(members, columns),
+        scratch_shapes=[pltpu.VMEM(x.shape, x.dtype) for x in inner] + frame(members, columns),
         compiler_params=room(20),
         name="outer",
     )(places, *pieces, *inner, coriolis)

time: 134 us -> 132 us (0.985)
  Pallas kernels: 23.1 us -> 20.4 us
    pallas_call x1, Pallas kernels: 8.1 us -> 5.54 us  [forecast(): pl.pallas_call(outer_kernel, out_shape=jax.ShapeDtypeStruct((blocks, 3 *...]
  transfers between devices with their start and end apart: 5 -> 5, of which waited for: 3 -> 3; matrix products, arithmetic and copies ran while one was open for 0% -> 1% of each run, Pallas kernels for 3% -> 3%
where the time goes in v3:
time: 132 us; the launch traced here: 131 us
  blocking collectives  57.4 us (43%)
  starting transfers between devices  25.7 us (19%)
  waiting for transfers between devices  25.6 us (19%)
  Pallas kernels  20.4 us (15%)
    all_to_all x1, blocking collectives, local(): returned = lax.all_to_all(result, MEM, 0, 0, tiled=True)  22.6 us
    all_to_all x1, waiting for transfers between devices, local(): gathered = lax.all_to_all(sent, MEM, 0, 0, tiled=True)  22.3 us
    all_to_all x1, blocking collectives, local(): pieces = lax.all_to_all(total_piece(parts, devices), MEM, 0, 0, tiled=True)  20.4 us
    all_to_all x1, blocking collectives, local(): parts = lax.all_to_all(parts, 'space', 0, 0, tiled=True)  14.5 us
    all_to_all x1, starting transfers between devices, local(): gathered = lax.all_to_all(sent, MEM, 0, 0, tiled=True)  10.2 us
    pallas_call x1, Pallas kernels, analysis(): pl.pallas_call(analysis_kernel, out_shape=jax.ShapeDtypeStruct((devices,...  8.77 us
    ppermute x1, starting transfers between devices, local(): after = lax.ppermute(planes, 'space', ring('space', -1))  8.49 us
    pallas_call x1, Pallas kernels, forecast(): pl.pallas_call(outer_kernel, out_shape=jax.ShapeDtypeStruct((blocks, 3 *...  5.54 us
  transfers between devices with their start and end apart: 5, of which 3 were waited for; matrix products, arithmetic and copies ran while one was open for 1% of the time, Pallas kernels for 3%

profile of v3, /device:TPU:8, one launch (start us, length us, event | category | flops | bytes accessed | tf_op | source)
XLA Modules:
  0.0 131.2 jit_solution(1485934428646013926)
XLA Ops:
  0.0 1.3 planes.1.own_ref
  1.3 0.0 collective-permute-start.1
  1.3 8.5 %collective-permute-start.2 = (f32[4,40,1024]{2,1,0:T(8,128)S(1)}, f32[4,40,1024]{2,1,0:T(8,128)S(1)}, u32[]{:S(2)}, u32[]{:S(2)}) collective-permute-start(f32[4,40,1024]{2,1,0:T(8,128)S(1)} %planes.1.own_ref), channel_id=1, source_target_pairs={{0,15},{1,0},{2,1},{3,2},{4,3},{5,4},{6,5},{7,6},{8,7},{9,8},{10,9... | collective-permute-start | bytes 1966088 | tf_op jit(solution)/shard_map/ppermute | solution.py:467
  9.8 0.1 fusion.2
  9.8 1.9 %collective-permute-start = (f32[2,40,1024]{2,1,0:T(8,128)S(1)}, f32[2,40,1024]{2,1,0:T(8,128)S(1)}, u32[]{:S(2)}, u32[]{:S(2)}) collective-permute-start(f32[2,40,1024]{2,1,0:T(8,128)S(1)} %get-tuple-element.10), channel_id=1, source_target_pairs={{0,2},{1,3},{2,4},{3,5},{4,6},{5,7},{6,8},{7,9},{8,10},{9,11},{10,... | collective-permute-start | bytes 983048 | tf_op jit(solution)/shard_map/ppermute | solution.py:468
  11.8 5.1 %collective-permute-start.3 = (f32[2,40,1024]{2,1,0:T(8,128)S(1)}, f32[2,40,1024]{2,1,0:T(8,128)S(1)}, u32[]{:S(2)}, u32[]{:S(2)}) collective-permute-start(f32[2,40,1024]{2,1,0:T(8,128)S(1)} %get-tuple-element.9), channel_id=1, source_target_pairs={{0,14},{1,15},{2,0},{3,1},{4,2},{5,3},{6,4},{7,5},{8,6},{9,7},{10,... | collective-permute-start | bytes 983048 | tf_op jit(solution)/shard_map/ppermute | solution.py:469
  16.9 0.7 and_select_fusion.3
  17.6 1.9 %collective-permute-done.1.before_ref = f32[4,40,1024]{2,1,0:T(8,128)S(1)} collective-permute-done((f32[4,40,1024]{2,1,0:T(8,128)S(1)}, f32[4,40,1024]{2,1,0:T(8,128)S(1)}, u32[]{:S(2)}, u32[]{:S(2)}) %collective-permute-start.1) | collective-permute-done | bytes 655392 | tf_op jit(solution)/shard_map/ppermute | solution.py:466
  19.5 1.4 %collective-permute-done.2.after_ref = f32[4,40,1024]{2,1,0:T(8,128)S(1)} collective-permute-done((f32[4,40,1024]{2,1,0:T(8,128)S(1)}, f32[4,40,1024]{2,1,0:T(8,128)S(1)}, u32[]{:S(2)}, u32[]{:S(2)}) %collective-permute-start.2) | collective-permute-done | bytes 655392 | tf_op jit(solution)/shard_map/ppermute | solution.py:467
  20.9 4.2 %inner.1 = (f32[3,16,12,1024]{3,2,1,0:T(8,128)S(1)}, f32[3,16,12,1024]{3,2,1,0:T(8,128)S(1)}) custom-call(f32[4,40,1024]{2,1,0:T(8,128)S(1)} %collective-permute-done.1.before_ref, f32[4,40,1024]{2,1,0:T(8,128)S(1)} %planes.1.own_ref, f32[4,40,1024]{2,1,0:T(8,128)S(1)} %collective-permute-done.2.after_ref, f32[1,1024]{1,0:T(1,128)S(1)} %multiply_add_fusion.coriolis_ref), custom_call_target="tpu_custom_call" | custom-call | tf_op jit(solution)/shard_map/inner/pallas_call | solution.py:252
  25.2 0.0 copy-start
  25.2 0.0 copy-start.1
  25.2 5.5 %outer.1 = f32[32,48,128]{2,1,0:T(8,128)} custom-call(s32[3,128]{1,0:T(4,128)S(1)} %pad_add_fusion.places, f32[2,40,1024]{2,1,0:T(8,128)S(1)} %collective-permute-done.far_before_ref, f32[4,40,1024]{2,1,0:T(8,128)S(1)} %collective-permute-done.1.before_ref, f32[4,40,1024]{2,1,0:T(8,128)S(1)} %planes.1.own_ref, ...), custom_call_target="tpu_custom_call" | custom-call | tf_op jit(solution)/shard_map/outer/pallas_call | solution.py:268
  30.7 10.2 %all-to-all-start = ((f32[32,48,128]{2,1,0:T(8,128)}), f32[32,48,128]{2,1,0:T(8,128)S(1)}, u32[]{:S(2)}, u32[]{:S(2)}) async-start(f32[32,48,128]{2,1,0:T(8,128)} %outer.1), calls=%async_computation | async-start | bytes 1572864 | tf_op jit(solution)/shard_map/all_to_all | solution.py:473
  40.9 22.3 %all-to-all-done.gathered_ref = f32[32,48,128]{2,1,0:T(8,128)S(1)} async-done(((f32[32,48,128]{2,1,0:T(8,128)}), f32[32,48,128]{2,1,0:T(8,128)S(1)}, u32[]{:S(2)}, u32[]{:S(2)}) %all-to-all-start) | async-done | bytes 786464 | tf_op jit(solution)/shard_map/all_to_all | solution.py:473
  63.2 0.6 gram.1
  63.8 14.5 %all_to_all.20.parts_ref = f32[16,5,4,128]{3,2,1,0:T(4,128)S(1)} all-to-all(f32[16,5,4,128]{3,2,1,0:T(4,128)S(1)} %gram.1), channel_id=1, replica_groups=mesh['mem_0'=8,'mem_1'=4,'space'=16] {'space'}, dimensions={0} | all-to-all | bytes 327680 | tf_op jit(solution)/shard_map/all_to_all | solution.py:475
  78.3 0.1 total.1
  78.4 20.4 %all_to_all.21 = f32[32,5,4,128]{3,2,1,0:T(4,128)S(1)} all-to-all(f32[32,5,4,128]{3,2,1,0:T(4,128)S(1)} %total.1), channel_id=1, replica_groups=mesh['mem_0'=8,'mem_1'=4,'space'=16] {'mem_0','mem_1'}, dimensions={0} | all-to-all | bytes 655360 | tf_op jit(solution)/shard_map/all_to_all | solution.py:476
  98.7 8.8 %analysis.1 = f32[32,9,4,128]{3,2,1,0:T(4,128)S(1)} custom-call(f32[160,4,128]{2,1,0:T(4,128)S(1)} %bitcast.9, f32[32,48,128]{2,1,0:T(8,128)S(1)} %all-to-all-done.gathered_ref), custom_call_target="tpu_custom_call" | custom-call | tf_op jit(solution)/shard_map/analysis/pallas_call | solution.py:436
  107.5 22.6 %all_to_all.22 = f32[32,9,4,128]{3,2,1,0:T(4,128)S(1)} all-to-all(f32[32,9,4,128]{3,2,1,0:T(4,128)S(1)} %analysis.1), channel_id=1, replica_groups=mesh['mem_0'=8,'mem_1'=4,'space'=16] {'mem_0','mem_1'}, dimensions={0} | all-to-all | bytes 1179648 | tf_op jit(solution)/shard_map/all_to_all | solution.py:478
  130.1 0.1 copy.8
  130.2 0.2 reshape.29
  130.4 0.9 copy.9
  (6 shorter events, 0.0 us)
Async XLA Ops:
  1.3 18.3 %collective-permute-start.1 = (f32[4,40,1024]{2,1,0:T(8,128)S(1)}, f32[4,40,1024]{2,1,0:T(8,128)S(1)}, u32[]{:S(2)}, u32[]{:S(2)}) collective-permute-start(f32[4,40,1024]{2,1,0:T(8,128)S(1)} %planes.1.own_ref), channel_id=1, source_target_pairs={{0,1},{1,2},{2,3},{3,4},{4,5},{5,6},{6,7},{7,8},{8,9},{9,10},{10,1... | collective-permute-start | bytes 1966088 | tf_op jit(solution)/shard_map/ppermute | solution.py:466
  1.3 19.6 %collective-permute-start.2 = (f32[4,40,1024]{2,1,0:T(8,128)S(1)}, f32[4,40,1024]{2,1,0:T(8,128)S(1)}, u32[]{:S(2)}, u32[]{:S(2)}) collective-permute-start(f32[4,40,1024]{2,1,0:T(8,128)S(1)} %planes.1.own_ref), channel_id=1, source_target_pairs={{0,15},{1,0},{2,1},{3,2},{4,3},{5,4},{6,5},{7,6},{8,7},{9,8},{10,9... | collective-permute-start | bytes 1966088 | tf_op jit(solution)/shard_map/ppermute | solution.py:467
  9.8 15.3 %collective-permute-start = (f32[2,40,1024]{2,1,0:T(8,128)S(1)}, f32[2,40,1024]{2,1,0:T(8,128)S(1)}, u32[]{:S(2)}, u32[]{:S(2)}) collective-permute-start(f32[2,40,1024]{2,1,0:T(8,128)S(1)} %get-tuple-element.10), channel_id=1, source_target_pairs={{0,2},{1,3},{2,4},{3,5},{4,6},{5,7},{6,8},{7,9},{8,10},{9,11},{10,... | collective-permute-start | bytes 983048 | tf_op jit(solution)/shard_map/ppermute | solution.py:468
  11.8 13.4 %collective-permute-start.3 = (f32[2,40,1024]{2,1,0:T(8,128)S(1)}, f32[2,40,1024]{2,1,0:T(8,128)S(1)}, u32[]{:S(2)}, u32[]{:S(2)}) collective-permute-start(f32[2,40,1024]{2,1,0:T(8,128)S(1)} %get-tuple-element.9), channel_id=1, source_target_pairs={{0,14},{1,15},{2,0},{3,1},{4,2},{5,3},{6,4},{7,5},{8,6},{9,7},{10,... | collective-permute-start | bytes 983048 | tf_op jit(solution)/shard_map/ppermute | solution.py:469
  25.2 38.0 %copy-start = (f32[1,128]{1,0:T(1,128)S(1)}, f32[1,128]{1,0:T(1,128)}, u32[]{:S(2)}) copy-start(f32[1,128]{1,0:T(1,128)} %value_ref.1) | copy-start | bytes 1540
  25.2 38.0 %copy-start.1 = (f32[1,128]{1,0:T(1,128)S(1)}, f32[1,128]{1,0:T(1,128)}, u32[]{:S(2)}) copy-start(f32[1,128]{1,0:T(1,128)} %error_ref.1) | copy-start | bytes 1540
  30.7 32.5 %all-to-all-start = ((f32[32,48,128]{2,1,0:T(8,128)}), f32[32,48,128]{2,1,0:T(8,128)S(1)}, u32[]{:S(2)}, u32[]{:S(2)}) async-start(f32[32,48,128]{2,1,0:T(8,128)} %outer.1), calls=%async_computation | async-start | bytes 1572864 | tf_op jit(solution)/shard_map/all_to_all | solution.py:473

commit v4 on v3

--- a/solution.py
+++ b/solution.py
@@ -99,14 +99,6 @@
     return [slice(at, min(at + 8, members)) for at in range(0, members, 8)]
 
 
-def repeat(first, last, row, unroll):
-    if unroll:
-        for r in range(first, last):
-            row(r, 0)
-    else:
-        lax.fori_loop(first, last, row, 0)
-
-
 def rows_of(ref, inner=None, first=0, last=-1):
     def get(f, r, m):
         return (inner if inner is not None and first <= r <= last else ref)[f, r, m]
@@ -114,10 +106,10 @@
     return get
 
 
-def advance(get, target, still, fresh_ref, coriolis, first, last, known=None, unroll=False):
+def advance(get, target, still, fresh_ref, coriolis, first, last, known=None):
     parts = sublane_parts(target.shape[2])
 
-    def height_row(r, carry):
+    def height_row(r):
         depth_above = still[r + 1, 0:1]
         depth_below = still[r - 1, 0:1]
         depth = still[r, 0:1]
@@ -129,13 +121,13 @@
             fresh_ref[r, m] = height - (0.5 * DT) * (
                 (above - below) + (north(across) - south(across))
             )
-        return carry
 
     low = first if known == first - 1 else first - 1
     high = last if known == last + 1 else last + 1
-    repeat(low, high + 1, height_row, unroll)
-
-    def flow_row(r, carry):
+    for r in range(low, high + 1):
+        height_row(r)
+
+    def flow_row(r):
         ocean = still[r, 1:2]
         for m in parts:
             u, v = get(1, r, m), get(2, r, m)
@@ -152,21 +144,17 @@
             tend = GRAV * (north(fresh) - south(fresh)) + u * (ve - vw) + v * (vn - vs)
             new = (1.0 - 4.0 * DT * VISC) * v - (0.5 * DT) * tend - coriolis * u
             target[2, r, m] = (new + (DT * VISC) * ((ve + vw) + (vn + vs))) * ocean
-        return carry
-
-    repeat(first, last + 1, flow_row, unroll)
+
+    for r in range(first, last + 1):
+        flow_row(r)
 
 
 def unpack(piece, count, at, state_ref, still_ref):
     members = state_ref.shape[2]
-
-    def row(r, carry):
+    for r in range(count):
         for f in range(3):
             state_ref[f, at + r] = piece[r, f * members : (f + 1) * members, :]
         still_ref[at + r] = piece[r, 3 * members : 3 * members + 2, :]
-        return carry
-
-    lax.fori_loop(0, count, row, 0)
 
 
 def inner_kernel(
@@ -208,13 +196,13 @@
     two = rows_of(b_ref, two_ref, 6, 9)
     for r in (4, 11):
         fresh_ref[r] = one_ref[0, r]
-    advance(raw, a_ref, still_ref, fresh_ref, coriolis, 2, 3, 4, True)
-    advance(raw, a_ref, still_ref, fresh_ref, coriolis, 12, 13, 11, True)
+    advance(raw, a_ref, still_ref, fresh_ref, coriolis, 2, 3, 4)
+    advance(raw, a_ref, still_ref, fresh_ref, coriolis, 12, 13, 11)
     for r in (6, 9):
         fresh_ref[r] = two_ref[0, r]
-    advance(one, b_ref, still_ref, fresh_ref, coriolis, 4, 5, 6, True)
-    advance(one, b_ref, still_ref, fresh_ref, coriolis, 10, 11, 9, True)
-    advance(two, raw_ref, still_ref, fresh_ref, coriolis, 6, 9, None, True)
+    advance(one, b_ref, still_ref, fresh_ref, coriolis, 4, 5, 6)
+    advance(one, b_ref, still_ref, fresh_ref, coriolis, 10, 11, 9)
+    advance(two, raw_ref, still_ref, fresh_ref, coriolis, 6, 9)
     source = raw_ref
     lane = lax.broadcasted_iota(jnp.int32, (members, LANES), 1)
 

time: 132 us -> 130 us (0.985)
  Pallas kernels: 20.4 us -> 18.1 us
  waiting for transfers between devices: 25.6 us -> 27.2 us
    pallas_call x1, Pallas kernels: 4.23 us -> 2.17 us  [inner_rows(): pl.pallas_call(inner_kernel, out_shape=(jax.ShapeDtypeStruct((3, 2 * HALO...]
    ppermute x1, waiting for transfers between devices: 0.01 us -> 1.37 us  [local(): far_after = lax.ppermute(planes[:edge], 'space', ring('space', -2))]
  transfers between devices with their start and end apart: 5 -> 5, of which waited for: 3 -> 5; matrix products, arithmetic and copies ran while one was open for 1% -> 1% of each run, Pallas kernels for 3% -> 2%
where the time goes in v4:
time: 130 us
  blocking collectives  56.6 us (44%)
  waiting for transfers between devices  27.2 us (21%)
  starting transfers between devices  25.7 us (20%)
  Pallas kernels  18.1 us (14%)
    all_to_all x1, blocking collectives, local(): returned = lax.all_to_all(result, MEM, 0, 0, tiled=True)  22.6 us
    all_to_all x1, waiting for transfers between devices, local(): gathered = lax.all_to_all(sent, MEM, 0, 0, tiled=True)  22.1 us
    all_to_all x1, blocking collectives, local(): pieces = lax.all_to_all(total_piece(parts, devices), MEM, 0, 0, tiled=True)  19.8 us
    all_to_all x1, blocking collectives, local(): parts = lax.all_to_all(parts, 'space', 0, 0, tiled=True)  14.3 us
    all_to_all x1, starting transfers between devices, local(): gathered = lax.all_to_all(sent, MEM, 0, 0, tiled=True)  10.2 us
    pallas_call x1, Pallas kernels, analysis(): pl.pallas_call(analysis_kernel, out_shape=jax.ShapeDtypeStruct((devices,...  8.77 us
    ppermute x1, starting transfers between devices, local(): after = lax.ppermute(planes, 'space', ring('space', -1))  8.49 us
    pallas_call x1, Pallas kernels, forecast(): pl.pallas_call(outer_kernel, out_shape=jax.ShapeDtypeStruct((blocks, 3 *...  5.3 us
  transfers between devices with their start and end apart: 5, of which 5 were waited for; matrix products, arithmetic and copies ran while one was open for 1% of the time, Pallas kernels for 2%

profile of v4, /device:TPU:8, one launch (start us, length us, event | category | flops | bytes accessed | tf_op | source)
XLA Modules:
  0.0 129.7 jit_solution(2208389921419155135)
XLA Ops:
  0.0 1.3 planes.1.own_ref
  1.3 0.0 collective-permute-start.1
  1.3 8.5 %collective-permute-start.2 = (f32[4,40,1024]{2,1,0:T(8,128)S(1)}, f32[4,40,1024]{2,1,0:T(8,128)S(1)}, u32[]{:S(2)}, u32[]{:S(2)}) collective-permute-start(f32[4,40,1024]{2,1,0:T(8,128)S(1)} %planes.1.own_ref), channel_id=1, source_target_pairs={{0,15},{1,0},{2,1},{3,2},{4,3},{5,4},{6,5},{7,6},{8,7},{9,8},{10,9... | collective-permute-start | bytes 1966088 | tf_op jit(solution)/shard_map/ppermute | solution.py:455
  9.8 0.1 fusion.2
  9.8 1.9 %collective-permute-start = (f32[2,40,1024]{2,1,0:T(8,128)S(1)}, f32[2,40,1024]{2,1,0:T(8,128)S(1)}, u32[]{:S(2)}, u32[]{:S(2)}) collective-permute-start(f32[2,40,1024]{2,1,0:T(8,128)S(1)} %get-tuple-element.10), channel_id=1, source_target_pairs={{0,2},{1,3},{2,4},{3,5},{4,6},{5,7},{6,8},{7,9},{8,10},{9,11},{10,... | collective-permute-start | bytes 983048 | tf_op jit(solution)/shard_map/ppermute | solution.py:456
  11.8 5.1 %collective-permute-start.3 = (f32[2,40,1024]{2,1,0:T(8,128)S(1)}, f32[2,40,1024]{2,1,0:T(8,128)S(1)}, u32[]{:S(2)}, u32[]{:S(2)}) collective-permute-start(f32[2,40,1024]{2,1,0:T(8,128)S(1)} %get-tuple-element.9), channel_id=1, source_target_pairs={{0,14},{1,15},{2,0},{3,1},{4,2},{5,3},{6,4},{7,5},{8,6},{9,7},{10,... | collective-permute-start | bytes 983048 | tf_op jit(solution)/shard_map/ppermute | solution.py:457
  16.9 0.7 and_select_fusion.3
  17.6 1.9 %collective-permute-done.1.before_ref = f32[4,40,1024]{2,1,0:T(8,128)S(1)} collective-permute-done((f32[4,40,1024]{2,1,0:T(8,128)S(1)}, f32[4,40,1024]{2,1,0:T(8,128)S(1)}, u32[]{:S(2)}, u32[]{:S(2)}) %collective-permute-start.1) | collective-permute-done | bytes 655392 | tf_op jit(solution)/shard_map/ppermute | solution.py:454
  19.5 1.4 %collective-permute-done.2.after_ref = f32[4,40,1024]{2,1,0:T(8,128)S(1)} collective-permute-done((f32[4,40,1024]{2,1,0:T(8,128)S(1)}, f32[4,40,1024]{2,1,0:T(8,128)S(1)}, u32[]{:S(2)}, u32[]{:S(2)}) %collective-permute-start.2) | collective-permute-done | bytes 655392 | tf_op jit(solution)/shard_map/ppermute | solution.py:455
  20.9 2.2 %inner.1 = (f32[3,16,12,1024]{3,2,1,0:T(8,128)S(1)}, f32[3,16,12,1024]{3,2,1,0:T(8,128)S(1)}) custom-call(f32[4,40,1024]{2,1,0:T(8,128)S(1)} %collective-permute-done.1.before_ref, f32[4,40,1024]{2,1,0:T(8,128)S(1)} %planes.1.own_ref, f32[4,40,1024]{2,1,0:T(8,128)S(1)} %collective-permute-done.2.after_ref, f32[1,1024]{1,0:T(1,128)S(1)} %multiply_add_fusion.coriolis_ref), custom_call_target="tpu_custom_call" | custom-call | tf_op jit(solution)/shard_map/inner/pallas_call | solution.py:240
  23.1 0.4 collective-permute-done.far_before_ref
  23.5 1.4 %collective-permute-done.3.far_after_ref = f32[2,40,1024]{2,1,0:T(8,128)S(1)} collective-permute-done((f32[2,40,1024]{2,1,0:T(8,128)S(1)}, f32[2,40,1024]{2,1,0:T(8,128)S(1)}, u32[]{:S(2)}, u32[]{:S(2)}) %collective-permute-start.3) | collective-permute-done | bytes 327712 | tf_op jit(solution)/shard_map/ppermute | solution.py:457
  24.9 5.3 %outer.1 = f32[32,48,128]{2,1,0:T(8,128)} custom-call(s32[3,128]{1,0:T(4,128)S(1)} %pad_add_fusion.places, f32[2,40,1024]{2,1,0:T(8,128)S(1)} %collective-permute-done.far_before_ref, f32[4,40,1024]{2,1,0:T(8,128)S(1)} %collective-permute-done.1.before_ref, f32[4,40,1024]{2,1,0:T(8,128)S(1)} %planes.1.own_ref, ...), custom_call_target="tpu_custom_call" | custom-call | tf_op jit(solution)/shard_map/outer/pallas_call | solution.py:256
  30.2 10.2 %all-to-all-start = ((f32[32,48,128]{2,1,0:T(8,128)}), f32[32,48,128]{2,1,0:T(8,128)S(1)}, u32[]{:S(2)}, u32[]{:S(2)}) async-start(f32[32,48,128]{2,1,0:T(8,128)} %outer.1), calls=%async_computation | async-start | bytes 1572864 | tf_op jit(solution)/shard_map/all_to_all | solution.py:461
  40.4 22.1 %all-to-all-done.gathered_ref = f32[32,48,128]{2,1,0:T(8,128)S(1)} async-done(((f32[32,48,128]{2,1,0:T(8,128)}), f32[32,48,128]{2,1,0:T(8,128)S(1)}, u32[]{:S(2)}, u32[]{:S(2)}) %all-to-all-start) | async-done | bytes 786464 | tf_op jit(solution)/shard_map/all_to_all | solution.py:461
  62.5 0.6 gram.1
  63.1 14.3 %all_to_all.20.parts_ref = f32[16,5,4,128]{3,2,1,0:T(4,128)S(1)} all-to-all(f32[16,5,4,128]{3,2,1,0:T(4,128)S(1)} %gram.1), channel_id=1, replica_groups=mesh['mem_0'=8,'mem_1'=4,'space'=16] {'space'}, dimensions={0} | all-to-all | bytes 327680 | tf_op jit(solution)/shard_map/all_to_all | solution.py:463
  77.3 0.1 total.1
  77.4 19.8 %all_to_all.21 = f32[32,5,4,128]{3,2,1,0:T(4,128)S(1)} all-to-all(f32[32,5,4,128]{3,2,1,0:T(4,128)S(1)} %total.1), channel_id=1, replica_groups=mesh['mem_0'=8,'mem_1'=4,'space'=16] {'mem_0','mem_1'}, dimensions={0} | all-to-all | bytes 655360 | tf_op jit(solution)/shard_map/all_to_all | solution.py:464
  97.2 8.8 %analysis.1 = f32[32,9,4,128]{3,2,1,0:T(4,128)S(1)} custom-call(f32[160,4,128]{2,1,0:T(4,128)S(1)} %bitcast.9, f32[32,48,128]{2,1,0:T(8,128)S(1)} %all-to-all-done.gathered_ref), custom_call_target="tpu_custom_call" | custom-call | tf_op jit(solution)/shard_map/analysis/pallas_call | solution.py:424
  105.9 22.6 %all_to_all.22 = f32[32,9,4,128]{3,2,1,0:T(4,128)S(1)} all-to-all(f32[32,9,4,128]{3,2,1,0:T(4,128)S(1)} %analysis.1), channel_id=1, replica_groups=mesh['mem_0'=8,'mem_1'=4,'space'=16] {'mem_0','mem_1'}, dimensions={0} | all-to-all | bytes 1179648 | tf_op jit(solution)/shard_map/all_to_all | solution.py:466
  128.5 0.1 copy.8
  128.6 0.2 reshape.29
  128.8 0.9 copy.9
  (6 shorter events, 0.0 us)
Async XLA Ops:
  1.3 18.3 %collective-permute-start.1 = (f32[4,40,1024]{2,1,0:T(8,128)S(1)}, f32[4,40,1024]{2,1,0:T(8,128)S(1)}, u32[]{:S(2)}, u32[]{:S(2)}) collective-permute-start(f32[4,40,1024]{2,1,0:T(8,128)S(1)} %planes.1.own_ref), channel_id=1, source_target_pairs={{0,1},{1,2},{2,3},{3,4},{4,5},{5,6},{6,7},{7,8},{8,9},{9,10},{10,1... | collective-permute-start | bytes 1966088 | tf_op jit(solution)/shard_map/ppermute | solution.py:454
  1.3 19.6 %collective-permute-start.2 = (f32[4,40,1024]{2,1,0:T(8,128)S(1)}, f32[4,40,1024]{2,1,0:T(8,128)S(1)}, u32[]{:S(2)}, u32[]{:S(2)}) collective-permute-start(f32[4,40,1024]{2,1,0:T(8,128)S(1)} %planes.1.own_ref), channel_id=1, source_target_pairs={{0,15},{1,0},{2,1},{3,2},{4,3},{5,4},{6,5},{7,6},{8,7},{9,8},{10,9... | collective-permute-start | bytes 1966088 | tf_op jit(solution)/shard_map/ppermute | solution.py:455
  9.8 13.7 %collective-permute-start = (f32[2,40,1024]{2,1,0:T(8,128)S(1)}, f32[2,40,1024]{2,1,0:T(8,128)S(1)}, u32[]{:S(2)}, u32[]{:S(2)}) collective-permute-start(f32[2,40,1024]{2,1,0:T(8,128)S(1)} %get-tuple-element.10), channel_id=1, source_target_pairs={{0,2},{1,3},{2,4},{3,5},{4,6},{5,7},{6,8},{7,9},{8,10},{9,11},{10,... | collective-permute-start | bytes 983048 | tf_op jit(solution)/shard_map/ppermute | solution.py:456
  11.8 13.1 %collective-permute-start.3 = (f32[2,40,1024]{2,1,0:T(8,128)S(1)}, f32[2,40,1024]{2,1,0:T(8,128)S(1)}, u32[]{:S(2)}, u32[]{:S(2)}) collective-permute-start(f32[2,40,1024]{2,1,0:T(8,128)S(1)} %get-tuple-element.9), channel_id=1, source_target_pairs={{0,14},{1,15},{2,0},{3,1},{4,2},{5,3},{6,4},{7,5},{8,6},{9,7},{10,... | collective-permute-start | bytes 983048 | tf_op jit(solution)/shard_map/ppermute | solution.py:457
  24.9 37.6 %copy-start = (f32[1,128]{1,0:T(1,128)S(1)}, f32[1,128]{1,0:T(1,128)}, u32[]{:S(2)}) copy-start(f32[1,128]{1,0:T(1,128)} %value_ref.1) | copy-start | bytes 1540
  24.9 37.6 %copy-start.1 = (f32[1,128]{1,0:T(1,128)S(1)}, f32[1,128]{1,0:T(1,128)}, u32[]{:S(2)}) copy-start(f32[1,128]{1,0:T(1,128)} %error_ref.1) | copy-start | bytes 1540
  30.2 32.2 %all-to-all-start = ((f32[32,48,128]{2,1,0:T(8,128)}), f32[32,48,128]{2,1,0:T(8,128)S(1)}, u32[]{:S(2)}, u32[]{:S(2)}) async-start(f32[32,48,128]{2,1,0:T(8,128)} %outer.1), calls=%async_computation | async-start | bytes 1572864 | tf_op jit(solution)/shard_map/all_to_all | solution.py:461

commit v5 on v4

--- a/solution.py
+++ b/solution.py
@@ -211,7 +211,7 @@
         block = source[0, HALO + places[0, o], :, pl.ds(start, LANES)]
         return jnp.where(lane == o, pltpu.roll(block, places[2, o], 1), found)
 
-    picks = lax.fori_loop(0, LANES, pick, jnp.zeros((members, LANES), jnp.float32), unroll=8)
+    picks = lax.fori_loop(0, LANES, pick, jnp.zeros((members, LANES), jnp.float32), unroll=32)
     per_row = columns // LANES
     spare = members // 3
     for f in range(3):

time: 130 us -> 129 us (level)
  no operation moved by 1% of the time
where the time goes in v5:
time: 129 us
  blocking collectives  56.6 us (44%)
  waiting for transfers between devices  27.2 us (21%)
  starting transfers between devices  25.7 us (20%)
  Pallas kernels  17.4 us (13%)
    all_to_all x1, blocking collectives, local(): returned = lax.all_to_all(result, MEM, 0, 0, tiled=True)  22.6 us
    all_to_all x1, waiting for transfers between devices, local(): gathered = lax.all_to_all(sent, MEM, 0, 0, tiled=True)  22.1 us
    all_to_all x1, blocking collectives, local(): pieces = lax.all_to_all(total_piece(parts, devices), MEM, 0, 0, tiled=True)  19.8 us
    all_to_all x1, blocking collectives, local(): parts = lax.all_to_all(parts, 'space', 0, 0, tiled=True)  14.3 us
    all_to_all x1, starting transfers between devices, local(): gathered = lax.all_to_all(sent, MEM, 0, 0, tiled=True)  10.2 us
    pallas_call x1, Pallas kernels, analysis(): pl.pallas_call(analysis_kernel, out_shape=jax.ShapeDtypeStruct((devices,...  8.77 us
    ppermute x1, starting transfers between devices, local(): after = lax.ppermute(planes, 'space', ring('space', -1))  8.49 us
    ppermute x1, starting transfers between devices, local(): far_after = lax.ppermute(planes[:edge], 'space', ring('space', -2))  5.13 us
  transfers between devices with their start and end apart: 5, of which 5 were waited for; matrix products, arithmetic and copies ran while one was open for 1% of the time, Pallas kernels for 2%

profile of v5, /device:TPU:8, one launch (start us, length us, event | category | flops | bytes accessed | tf_op | source)
XLA Modules:
  0.0 128.9 jit_solution(4282592632347208781)
XLA Ops:
  0.0 1.3 planes.1.own_ref
  1.3 0.0 collective-permute-start.1
  1.3 8.5 %collective-permute-start.2 = (f32[4,40,1024]{2,1,0:T(8,128)S(1)}, f32[4,40,1024]{2,1,0:T(8,128)S(1)}, u32[]{:S(2)}, u32[]{:S(2)}) collective-permute-start(f32[4,40,1024]{2,1,0:T(8,128)S(1)} %planes.1.own_ref), channel_id=1, source_target_pairs={{0,15},{1,0},{2,1},{3,2},{4,3},{5,4},{6,5},{7,6},{8,7},{9,8},{10,9... | collective-permute-start | bytes 1966088 | tf_op jit(solution)/shard_map/ppermute | solution.py:455
  9.8 0.1 fusion.2
  9.8 1.9 %collective-permute-start = (f32[2,40,1024]{2,1,0:T(8,128)S(1)}, f32[2,40,1024]{2,1,0:T(8,128)S(1)}, u32[]{:S(2)}, u32[]{:S(2)}) collective-permute-start(f32[2,40,1024]{2,1,0:T(8,128)S(1)} %get-tuple-element.10), channel_id=1, source_target_pairs={{0,2},{1,3},{2,4},{3,5},{4,6},{5,7},{6,8},{7,9},{8,10},{9,11},{10,... | collective-permute-start | bytes 983048 | tf_op jit(solution)/shard_map/ppermute | solution.py:456
  11.8 5.1 %collective-permute-start.3 = (f32[2,40,1024]{2,1,0:T(8,128)S(1)}, f32[2,40,1024]{2,1,0:T(8,128)S(1)}, u32[]{:S(2)}, u32[]{:S(2)}) collective-permute-start(f32[2,40,1024]{2,1,0:T(8,128)S(1)} %get-tuple-element.9), channel_id=1, source_target_pairs={{0,14},{1,15},{2,0},{3,1},{4,2},{5,3},{6,4},{7,5},{8,6},{9,7},{10,... | collective-permute-start | bytes 983048 | tf_op jit(solution)/shard_map/ppermute | solution.py:457
  16.9 0.7 and_select_fusion.3
  17.6 1.9 %collective-permute-done.1.before_ref = f32[4,40,1024]{2,1,0:T(8,128)S(1)} collective-permute-done((f32[4,40,1024]{2,1,0:T(8,128)S(1)}, f32[4,40,1024]{2,1,0:T(8,128)S(1)}, u32[]{:S(2)}, u32[]{:S(2)}) %collective-permute-start.1) | collective-permute-done | bytes 655392 | tf_op jit(solution)/shard_map/ppermute | solution.py:454
  19.5 1.4 %collective-permute-done.2.after_ref = f32[4,40,1024]{2,1,0:T(8,128)S(1)} collective-permute-done((f32[4,40,1024]{2,1,0:T(8,128)S(1)}, f32[4,40,1024]{2,1,0:T(8,128)S(1)}, u32[]{:S(2)}, u32[]{:S(2)}) %collective-permute-start.2) | collective-permute-done | bytes 655392 | tf_op jit(solution)/shard_map/ppermute | solution.py:455
  20.9 2.2 %inner.1 = (f32[3,16,12,1024]{3,2,1,0:T(8,128)S(1)}, f32[3,16,12,1024]{3,2,1,0:T(8,128)S(1)}) custom-call(f32[4,40,1024]{2,1,0:T(8,128)S(1)} %collective-permute-done.1.before_ref, f32[4,40,1024]{2,1,0:T(8,128)S(1)} %planes.1.own_ref, f32[4,40,1024]{2,1,0:T(8,128)S(1)} %collective-permute-done.2.after_ref, f32[1,1024]{1,0:T(1,128)S(1)} %multiply_add_fusion.coriolis_ref), custom_call_target="tpu_custom_call" | custom-call | tf_op jit(solution)/shard_map/inner/pallas_call | solution.py:240
  23.1 0.4 collective-permute-done.far_before_ref
  23.5 1.4 %collective-permute-done.3.far_after_ref = f32[2,40,1024]{2,1,0:T(8,128)S(1)} collective-permute-done((f32[2,40,1024]{2,1,0:T(8,128)S(1)}, f32[2,40,1024]{2,1,0:T(8,128)S(1)}, u32[]{:S(2)}, u32[]{:S(2)}) %collective-permute-start.3) | collective-permute-done | bytes 327712 | tf_op jit(solution)/shard_map/ppermute | solution.py:457
  24.9 4.6 %outer.1 = f32[32,48,128]{2,1,0:T(8,128)} custom-call(s32[3,128]{1,0:T(4,128)S(1)} %pad_add_fusion.places, f32[2,40,1024]{2,1,0:T(8,128)S(1)} %collective-permute-done.far_before_ref, f32[4,40,1024]{2,1,0:T(8,128)S(1)} %collective-permute-done.1.before_ref, f32[4,40,1024]{2,1,0:T(8,128)S(1)} %planes.1.own_ref, ...), custom_call_target="tpu_custom_call" | custom-call | tf_op jit(solution)/shard_map/outer/pallas_call | solution.py:256
  29.5 10.2 %all-to-all-start = ((f32[32,48,128]{2,1,0:T(8,128)}), f32[32,48,128]{2,1,0:T(8,128)S(1)}, u32[]{:S(2)}, u32[]{:S(2)}) async-start(f32[32,48,128]{2,1,0:T(8,128)} %outer.1), calls=%async_computation | async-start | bytes 1572864 | tf_op jit(solution)/shard_map/all_to_all | solution.py:461
  39.7 22.1 %all-to-all-done.gathered_ref = f32[32,48,128]{2,1,0:T(8,128)S(1)} async-done(((f32[32,48,128]{2,1,0:T(8,128)}), f32[32,48,128]{2,1,0:T(8,128)S(1)}, u32[]{:S(2)}, u32[]{:S(2)}) %all-to-all-start) | async-done | bytes 786464 | tf_op jit(solution)/shard_map/all_to_all | solution.py:461
  61.7 0.6 gram.1
  62.3 14.3 %all_to_all.20.parts_ref = f32[16,5,4,128]{3,2,1,0:T(4,128)S(1)} all-to-all(f32[16,5,4,128]{3,2,1,0:T(4,128)S(1)} %gram.1), channel_id=1, replica_groups=mesh['mem_0'=8,'mem_1'=4,'space'=16] {'space'}, dimensions={0} | all-to-all | bytes 327680 | tf_op jit(solution)/shard_map/all_to_all | solution.py:463
  76.6 0.1 total.1
  76.7 19.8 %all_to_all.21 = f32[32,5,4,128]{3,2,1,0:T(4,128)S(1)} all-to-all(f32[32,5,4,128]{3,2,1,0:T(4,128)S(1)} %total.1), channel_id=1, replica_groups=mesh['mem_0'=8,'mem_1'=4,'space'=16] {'mem_0','mem_1'}, dimensions={0} | all-to-all | bytes 655360 | tf_op jit(solution)/shard_map/all_to_all | solution.py:464
  96.5 8.8 %analysis.1 = f32[32,9,4,128]{3,2,1,0:T(4,128)S(1)} custom-call(f32[160,4,128]{2,1,0:T(4,128)S(1)} %bitcast.9, f32[32,48,128]{2,1,0:T(8,128)S(1)} %all-to-all-done.gathered_ref), custom_call_target="tpu_custom_call" | custom-call | tf_op jit(solution)/shard_map/analysis/pallas_call | solution.py:424
  105.2 22.6 %all_to_all.22 = f32[32,9,4,128]{3,2,1,0:T(4,128)S(1)} all-to-all(f32[32,9,4,128]{3,2,1,0:T(4,128)S(1)} %analysis.1), channel_id=1, replica_groups=mesh['mem_0'=8,'mem_1'=4,'space'=16] {'mem_0','mem_1'}, dimensions={0} | all-to-all | bytes 1179648 | tf_op jit(solution)/shard_map/all_to_all | solution.py:466
  127.8 0.1 copy.8
  127.9 0.2 reshape.29
  128.1 0.9 copy.9
  (6 shorter events, 0.0 us)
Async XLA Ops:
  1.3 18.3 %collective-permute-start.1 = (f32[4,40,1024]{2,1,0:T(8,128)S(1)}, f32[4,40,1024]{2,1,0:T(8,128)S(1)}, u32[]{:S(2)}, u32[]{:S(2)}) collective-permute-start(f32[4,40,1024]{2,1,0:T(8,128)S(1)} %planes.1.own_ref), channel_id=1, source_target_pairs={{0,1},{1,2},{2,3},{3,4},{4,5},{5,6},{6,7},{7,8},{8,9},{9,10},{10,1... | collective-permute-start | bytes 1966088 | tf_op jit(solution)/shard_map/ppermute | solution.py:454
  1.3 19.6 %collective-permute-start.2 = (f32[4,40,1024]{2,1,0:T(8,128)S(1)}, f32[4,40,1024]{2,1,0:T(8,128)S(1)}, u32[]{:S(2)}, u32[]{:S(2)}) collective-permute-start(f32[4,40,1024]{2,1,0:T(8,128)S(1)} %planes.1.own_ref), channel_id=1, source_target_pairs={{0,15},{1,0},{2,1},{3,2},{4,3},{5,4},{6,5},{7,6},{8,7},{9,8},{10,9... | collective-permute-start | bytes 1966088 | tf_op jit(solution)/shard_map/ppermute | solution.py:455
  9.8 13.7 %collective-permute-start = (f32[2,40,1024]{2,1,0:T(8,128)S(1)}, f32[2,40,1024]{2,1,0:T(8,128)S(1)}, u32[]{:S(2)}, u32[]{:S(2)}) collective-permute-start(f32[2,40,1024]{2,1,0:T(8,128)S(1)} %get-tuple-element.10), channel_id=1, source_target_pairs={{0,2},{1,3},{2,4},{3,5},{4,6},{5,7},{6,8},{7,9},{8,10},{9,11},{10,... | collective-permute-start | bytes 983048 | tf_op jit(solution)/shard_map/ppermute | solution.py:456
  11.8 13.1 %collective-permute-start.3 = (f32[2,40,1024]{2,1,0:T(8,128)S(1)}, f32[2,40,1024]{2,1,0:T(8,128)S(1)}, u32[]{:S(2)}, u32[]{:S(2)}) collective-permute-start(f32[2,40,1024]{2,1,0:T(8,128)S(1)} %get-tuple-element.9), channel_id=1, source_target_pairs={{0,14},{1,15},{2,0},{3,1},{4,2},{5,3},{6,4},{7,5},{8,6},{9,7},{10,... | collective-permute-start | bytes 983048 | tf_op jit(solution)/shard_map/ppermute | solution.py:457
  24.9 36.8 %copy-start = (f32[1,128]{1,0:T(1,128)S(1)}, f32[1,128]{1,0:T(1,128)}, u32[]{:S(2)}) copy-start(f32[1,128]{1,0:T(1,128)} %value_ref.1) | copy-start | bytes 1540
  24.9 36.8 %copy-start.1 = (f32[1,128]{1,0:T(1,128)S(1)}, f32[1,128]{1,0:T(1,128)}, u32[]{:S(2)}) copy-start(f32[1,128]{1,0:T(1,128)} %error_ref.1) | copy-start | bytes 1540
  29.5 32.2 %all-to-all-start = ((f32[32,48,128]{2,1,0:T(8,128)}), f32[32,48,128]{2,1,0:T(8,128)S(1)}, u32[]{:S(2)}, u32[]{:S(2)}) async-start(f32[32,48,128]{2,1,0:T(8,128)} %outer.1), calls=%async_computation | async-start | bytes 1572864 | tf_op jit(solution)/shard_map/all_to_all | solution.py:461
